TPU v7x, 32 devices: a 4x4x1 block of a 4x4x8 slice. The times are simulated.
32 devices in a mesh: data: 1 (over z), col: 4 (over y), row: 8 (over x, core).
Axes of the slice: x: 4, y: 4, z: 1, core: 2. Of those that a mesh axis runs over, the one named last changes fastest.
The devices are a block of a 4x4x8 slice.
Arguments:
- residual: bfloat16 [4096, 4096], P('data', 'row')
- gain_mlp: float32 [4096], P('row')
- gain_attn: float32 [4096], P('row')
- w_gate: bfloat16 [4096, 16384], P(None, ('col', 'row'))
- w_up: bfloat16 [4096, 16384], P(None, ('col', 'row'))
- w_down: bfloat16 [16384, 4096], P('col', 'row')
- w_qkv: bfloat16 [4096, 4608], P(None, ('col', 'row'))
Outputs:
- output 1: bfloat16 [4096, 4096], P('data', 'row')
- output 2: bfloat16 [4096, 4608], P('data', ('col', 'row'))
All inputs are finite; a program needn't handle non-finite values.
Results may differ from a plain program's by a relative error of at most 0.00402297.
Values are sent between devices in bfloat16 or wider.
A program may use at most 768 MiB of HBM per device.

v0:
```python
import jax
import jax.numpy as jnp
from jax import lax
from jax.sharding import PartitionSpec as P

NORM_EPS = 1e-6


def solution(mesh):
    row_size = mesh.shape['row']
    tok_spec = P('data', 'row')
    gain_spec = P('row')
    wide_spec = P(None, ('col', 'row'))
    down_spec = P('col', 'row')
    qkv_spec = P('data', ('col', 'row'))

    def shard_norm(shard, gain):
        shard_f = shard.astype(jnp.float32)
        sq_part = jnp.sum(shard_f * shard_f, axis=1, keepdims=True)
        sq_total = lax.psum(sq_part, 'row')
        row_scale = lax.rsqrt(sq_total / (shard.shape[1] * row_size) + NORM_EPS)
        return (shard_f * row_scale * gain).astype(jnp.bfloat16)

    def per_device(residual, gain_mlp, gain_attn, w_gate, w_up, w_down, w_qkv):
        normed = shard_norm(residual, gain_mlp)
        normed_full = lax.all_gather(normed, 'row', axis=1, tiled=True)
        gate_val = jnp.dot(normed_full, w_gate, preferred_element_type=jnp.float32)
        up_val = jnp.dot(normed_full, w_up, preferred_element_type=jnp.float32)
        act_val = (jax.nn.silu(gate_val) * up_val).astype(jnp.bfloat16)
        act_block = lax.all_gather(act_val, 'row', axis=1, tiled=True)
        down_part = jnp.dot(act_block, w_down, preferred_element_type=jnp.float32)
        down_sum = lax.psum(down_part, 'col')
        resid_next = (residual.astype(jnp.float32) + down_sum).astype(jnp.bfloat16)
        normed_next = shard_norm(resid_next, gain_attn)
        next_full = lax.all_gather(normed_next, 'row', axis=1, tiled=True)
        qkv_out = jnp.dot(next_full, w_qkv, preferred_element_type=jnp.float32).astype(jnp.bfloat16)
        return resid_next, qkv_out

    return jax.shard_map(per_device, mesh=mesh, in_specs=(tok_spec, gain_spec, gain_spec, wide_spec, wide_spec, down_spec, wide_spec), out_specs=(tok_spec, qkv_spec), check_vma=False)
```

profile of v0, /device:TPU:97, one launch (start us, length us, event | category | flops | bytes accessed | tf_op | source)
XLA Modules:
  0.0 794.2 jit_solution(10284847003373431273)
XLA Ops:
  7.2 0.0 copy-start
  7.2 0.1 all-gather.4.cloned.1.call-start
  7.3 3.2 fusion.3
  10.4 24.0 %psum.21 = f32[4096,1]{0,1:T(1,128)S(1)} all-reduce(f32[4096,1]{0,1:T(1,128)S(1)} %bitcast.15), channel_id=1, replica_groups=mesh['data'=1,'col'=4,'row'=8] {'row'}, use_global_device_ids=true, to_apply=%region_1.0 | all-reduce | flops 4096 | bytes 32768 | tf_op jit(solution)/shard_map/psum | solution.py:20
  34.5 4.2 fusion.5
  38.6 0.1 all-gather.4.cloned.1.call-update
  38.7 0.1 all-gather.6.cloned.1.call-start
  38.8 158.0 %all-gather.4.cloned.1.call-done = bf16[4096,4096]{1,0:T(8,128)(2,1)} async-done(((bf16[4096,512]{1,0:T(8,128)(2,1)}), bf16[4096,4096]{1,0:T(8,128)(2,1)}) %all-gather.4.cloned.1.call-update) | async-done | bytes 33554448 | tf_op jit(solution)/shard_map/all_gather | solution.py:26
  196.7 0.0 copy-start.2
  196.8 22.7 %fusion.8 = f32[4096,512]{1,0:T(8,128)S(1)} fusion(bf16[4096,4096]{1,0:T(8,128)(2,1)} %all-gather.4.cloned.1.call-done, bf16[4096,512]{1,0:T(8,128)(2,1)} %param.10), kind=kOutput, calls=%fused_computation.16 | convolution fusion | flops 17179869184 | bytes 46137344 | tf_op jit(solution)/shard_map/dot_general | solution.py:27
  219.5 0.0 copy-done.2
  219.5 24.5 %multiply_convert_fusion = bf16[4096,512]{1,0:T(8,128)(2,1)} fusion(f32[4096,512]{1,0:T(8,128)S(1)} %fusion.8, bf16[4096,4096]{1,0:T(8,128)(2,1)} %all-gather.4.cloned.1.call-done, bf16[4096,512]{1,0:T(8,128)(2,1)S(1)} %copy-done.2), kind=kOutput, calls=%fused_computation.12 | convolution fusion | flops 17192452096 | bytes 50331648 | tf_op jit(solution)/shard_map/dot_general | solution.py:28
  244.0 0.1 all-gather.6.cloned.1.call-update
  244.0 0.2 all-reduce.2.cloned.1.call-start
  244.3 155.0 %all-gather.6.cloned.1.call-done = bf16[4096,4096]{1,0:T(8,128)(2,1)} async-done(((bf16[4096,512]{1,0:T(8,128)(2,1)}), bf16[4096,4096]{1,0:T(8,128)(2,1)}) %all-gather.6.cloned.1.call-update) | async-done | bytes 33554448 | tf_op jit(solution)/shard_map/all_gather | solution.py:30
  399.3 24.9 %fusion.9 = f32[4096,512]{1,0:T(8,128)} fusion(bf16[4096,4096]{1,0:T(8,128)(2,1)} %all-gather.6.cloned.1.call-done, bf16[4096,512]{1,0:T(8,128)(2,1)} %param.12), kind=kOutput, calls=%fused_computation.17 | convolution fusion | flops 17179869184 | bytes 46137344 | tf_op jit(solution)/shard_map/dot_general | solution.py:31
  424.2 0.1 all-reduce.2.cloned.1.call-update
  424.2 0.0 copy-start.1
  424.2 0.1 all-gather.8.cloned.1.call-start
  424.3 155.3 %all-reduce.2.cloned.1.call-done = f32[4096,512]{1,0:T(8,128)} async-done(((f32[4096,512]{1,0:T(8,128)}), f32[4096,512]{1,0:T(8,128)}) %all-reduce.2.cloned.1.call-update) | async-done | bytes 8388624 | tf_op jit(solution)/shard_map/psum | solution.py:32
  579.6 7.8 fusion
  587.4 22.7 %psum.23 = f32[4096,1]{0,1:T(1,128)S(1)} all-reduce(f32[4096,1]{0,1:T(1,128)S(1)} %bitcast.12), channel_id=1, replica_groups=mesh['data'=1,'col'=4,'row'=8] {'row'}, use_global_device_ids=true, to_apply=%region_4.5 | all-reduce | flops 4096 | bytes 32768 | tf_op jit(solution)/shard_map/psum | solution.py:20
  610.1 0.0 copy-done.1
  610.1 4.2 fusion.2
  614.3 0.1 all-gather.8.cloned.1.call-update
  614.4 155.0 %all-gather.8.cloned.1.call-done = bf16[4096,4096]{1,0:T(8,128)(2,1)} async-done(((bf16[4096,512]{1,0:T(8,128)(2,1)}), bf16[4096,4096]{1,0:T(8,128)(2,1)}) %all-gather.8.cloned.1.call-update) | async-done | bytes 33554448 | tf_op jit(solution)/shard_map/all_gather | solution.py:35
  769.4 0.0 copy-done
  769.4 18.3 %convolution_convert_fusion = bf16[4096,144]{0,1:T(8,128)(2,1)} fusion(bf16[4096,4096]{1,0:T(8,128)(2,1)} %all-gather.8.cloned.1.call-done, bf16[4096,144]{0,1:T(8,128)(2,1)S(1)} %copy-done), kind=kOutput, calls=%fused_computation.13 | convolution fusion | flops 4832428032 | bytes 35913728 | tf_op jit(solution)/shard_map/dot_general | solution.py:36
  (2 shorter events, 0.1 us)
Async XLA Ops:
  7.2 762.2 %copy-start = (bf16[4096,144]{0,1:T(8,128)(2,1)S(1)}, bf16[4096,144]{0,1:T(8,128)(2,1)}, u32[]{:S(2)}) copy-start(bf16[4096,144]{0,1:T(8,128)(2,1)} %param.13) | copy-start | bytes 3538948
  7.2 189.6 %all-gather.4.cloned.1.call-start = ((), (), s32[]{:S(2)}) async-start(), calls=%async_computation | async-start | bytes 37748736 | tf_op jit(solution)/shard_map/all_gather | solution.py:26
  38.7 360.6 %all-gather.6.cloned.1.call-start = ((), (), s32[]{:S(2)}) async-start(), calls=%async_computation.1 | async-start | bytes 37748736 | tf_op jit(solution)/shard_map/all_gather | solution.py:30
  196.7 22.7 %copy-start.2 = (bf16[4096,512]{1,0:T(8,128)(2,1)S(1)}, bf16[4096,512]{1,0:T(8,128)(2,1)}, u32[]{:S(2)}) copy-start(bf16[4096,512]{1,0:T(8,128)(2,1)} %param.11) | copy-start | bytes 12582916
  244.0 335.6 %all-reduce.2.cloned.1.call-start = ((), (), s32[]{:S(2)}) async-start(), calls=%async_computation.2 | async-start | bytes 16777216 | tf_op jit(solution)/shard_map/psum | solution.py:32
  424.2 185.9 %copy-start.1 = (f32[512]{0:T(512)S(1)}, f32[512]{0:T(512)}, u32[]{:S(2)}) copy-start(f32[512]{0:T(512)} %param.9) | copy-start | bytes 6148
  424.2 345.1 %all-gather.8.cloned.1.call-start = ((), (), s32[]{:S(2)}) async-start(), calls=%async_computation.3 | async-start | bytes 37748736 | tf_op jit(solution)/shard_map/all_gather | solution.py:35
Sparse Core Ops, SparseCore 0:
  38.8 157.8 all-gather.3
  244.1 155.0 all-gather.5
  424.3 155.1 all-reduce.1
  614.5 154.8 all-gather.7
where the time goes:
time: 794 us
  waiting for transfers between devices  623 us (78%)
  matrix products  90.3 us (11%)
  blocking collectives  46.7 us (6%)
  other arithmetic  19.4 us (2%)
  between operations  13.8 us (2%)
    all_gather x1, waiting for transfers between devices, per_device(): normed_full = lax.all_gather(normed, 'row', axis=1, tiled=True)  158 us
    psum x1, waiting for transfers between devices, per_device(): down_sum = lax.psum(down_part, 'col')  155 us
    all_gather x1, waiting for transfers between devices, per_device(): act_block = lax.all_gather(act_val, 'row', axis=1, tiled=True)  155 us
    all_gather x1, waiting for transfers between devices, per_device(): next_full = lax.all_gather(normed_next, 'row', axis=1, tiled=True)  155 us
    psum x2, blocking collectives, shard_norm(): sq_total = lax.psum(sq_part, 'row')  46.7 us
    dot_general x1, matrix products, per_device(): down_part = jnp.dot(act_block, w_down, preferred_element_type=jnp.float32)  24.9 us
    dot_general x1, matrix products, per_device(): up_val = jnp.dot(normed_full, w_up, preferred_element_type=jnp.float32)  24.5 us
    dot_general x1, matrix products, per_device(): gate_val = jnp.dot(normed_full, w_gate, preferred_element_type=jnp.float32)  22.7 us
  transfers between devices with their start and end apart: 4, of which 4 were waited for; matrix products, arithmetic and copies ran while one was open for 0% of the time, Pallas kernels for 0%

commit v1 on v0

v1 whole, which is shorter than its diff:
```python
import functools

import jax
import jax.numpy as jnp
from jax import lax
from jax.experimental import pallas as pl
from jax.experimental.pallas import tpu as pltpu
from jax.sharding import PartitionSpec as P

NORM_EPS = 1e-6
MESH = pl.DeviceIdType.MESH
BF16 = jnp.bfloat16
F32 = jnp.float32
ANY = pl.BlockSpec(memory_space=pl.ANY)
VMEM = pl.BlockSpec(memory_space=pltpu.VMEM)
DMA = pltpu.SemaphoreType.DMA
LIMIT = 64 * 1024 * 1024 - 128 * 1024

NX, NY = 4, 4
SY = 5
SX = 12
SY_CHUNKS = ((0, 1), (1, 2), (3, 2))
SX_CHUNKS = tuple((i, 2) for i in range(0, SX, 2))
PIECES = NY * SY + SX


def place():
    row, y = lax.axis_index("row"), lax.axis_index("col")
    return lax.div(row, 2), lax.rem(row, 2), row, y


def around(i, n):
    return lax.rem(i + 1, n), lax.rem(i + n - 1, n), lax.rem(i + 2, n)


def greet(peers):
    barrier = pltpu.get_barrier_semaphore()
    for row, y in peers:
        pl.semaphore_signal(barrier, inc=1, device_id={"row": row, "col": y}, device_id_type=MESH)
    pl.semaphore_wait(barrier, len(peers))


def to(src, dst, send, recv, row, y):
    return pltpu.make_async_remote_copy(src, dst, send, recv, device_id={"row": row, "col": y}, device_id_type=MESH)


def norm_rows(load, gains, which, store, n_ent, width):
    acc = None
    for e in range(n_ent):
        v = load(e).astype(F32)
        acc = v * v if acc is None else acc + v * v
    scale = lax.rsqrt(jnp.sum(acc, axis=1, keepdims=True) / (n_ent * width) + NORM_EPS)
    for e in range(n_ent):
        store(e, (load(e).astype(F32) * scale * gains[e, which : which + 1, :]).astype(BF16))


def k1_names():
    names = []
    for k in range(len(SY_CHUNKS)):
        names += [f"{n}_{k}" for n in ("xp", "xm", "xpf", "xmf", "yp1", "yp2", "yp3", "ym1", "ym2", "ym3")]
        names += [f"{n}_{k}" for n in ("ypf1", "ypf3", "ymf2", "ymf3")]
    for k in range(len(SX_CHUNKS)):
        names += [f"{n}_{k}" for n in ("sp", "sm", "spf", "smf")]
    names += [f"d_{s}" for s in range(NY + 1)]
    names += [f"g_{d}" for d in range(1, 2 * NX)]
    names += ["wg", "wu"]
    return names


K1_TILES = (
    (("s", 0), ("s", 1)),
    (("s", 2), ("m", 0)),
    (("p", 0), ("s", 3)),
    (("s", 4), ("m", 1)),
    (("m", 2), ("p", 1)),
    (("p", 2), ("x", 0)),
    (("x", 1), ("o", 0)),
    (("x", 2), ("x", 3)),
    (("x", 4), ("x", 5)),
    (("m", 3), ("m", 4)),
    (("p", 3), ("p", 4)),
    (("o", 1), ("o", 2)),
    (("x", 6), ("x", 7)),
    (("x", 8), ("x", 9)),
    (("o", 3), ("o", 4)),
    (("x", 10), ("x", 11)),
)


def k1_plan():
    both = lambda n, k: [f"{n}p_{k}", f"{n}m_{k}"]
    bothf = lambda n, k: [f"{n}pf_{k}", f"{n}mf_{k}"]
    ypair = lambda k: [f"{n}_{k}" for n in ("yp1", "yp2", "ym1", "ym2")]
    ytrip = lambda k: [f"{n}_{k}" for n in ("yp3", "ym3")]
    yfwd = lambda k: [f"{n}_{k}" for n in ("ypf1", "ypf3", "ymf2", "ymf3")]
    w, s = "w", "s"
    return {
        -1: [
            (s, both("x", 0) + both("x", 1)),
            (w, both("x", 0)),
            (s, bothf("x", 0) + ypair(0) + both("x", 2)),
            (w, bothf("x", 0)),
            (s, ytrip(0)),
            (w, both("x", 1)),
            (s, bothf("x", 1) + ypair(1)),
            ("rest", []),
            (s, both("s", 0)),
            (w, both("x", 2)),
            (s, bothf("x", 2) + both("s", 1)),
            (w, bothf("x", 1)),
            (s, ytrip(1)),
        ],
        1: [(w, ypair(0) + ytrip(0)), (s, yfwd(0))],
        2: [
            (w, bothf("x", 2)),
            (s, ypair(2) + ytrip(2)),
            (w, both("s", 0)),
            (s, bothf("s", 0) + both("s", 2)),
        ],
        3: [(w, ypair(1) + ytrip(1)), (s, yfwd(1))],
        4: [(w, both("s", 1)), (s, bothf("s", 1) + both("s", 3))],
        5: [(w, bothf("s", 0))],
        6: [(w, yfwd(0))],
        7: [(w, bothf("s", 1) + both("s", 2)), (s, bothf("s", 2) + both("s", 4))],
        8: [(w, bothf("s", 2) + both("s", 3)), (s, bothf("s", 3) + both("s", 5))],
        9: [(w, ypair(2) + ytrip(2)), (s, yfwd(2))],
        10: [(w, both("s", 4)), (s, bothf("s", 4))],
        11: [(w, yfwd(1))],
        12: [(w, bothf("s", 3) + both("s", 5)), (s, bothf("s", 5))],
        13: [(w, bothf("s", 4))],
        14: [(w, yfwd(2))],
        15: [(w, bothf("s", 5))],
    }


def k1(x_ref, g_ref, wg_ref, wu_ref, a_ref, xres_ref, gout_ref, xb, wgb, wub, nt, gb, send, recv, loc):
    x, c, row, y = place()
    xp, xm, x2 = around(x, NX)
    yp, ym, y2 = around(y, NY)
    n_ent = 2 * NX
    half, width, ff = xb.shape[1], xb.shape[2], wgb.shape[2]
    piece = half // PIECES
    ids = {n: i for i, n in enumerate(k1_names())}
    partner = 2 * x + 1 - c

    copies = {}

    def define(name, src, dst, to_row, to_y):
        i = ids[name]
        copies[name] = to(src, dst, send.at[i], recv.at[i], to_row, to_y)

    def ring(name, ents, rows, to_row, to_y):
        ref = xb.at[ents, rows]
        define(name, ref, ref, to_row, to_y)

    blk = lambda i: pl.ds(2 * i, 2)
    ent = lambda i: pl.ds(i, 1)
    row_p, row_m = 2 * xp + c, 2 * xm + c
    for k, (o, n) in enumerate(SY_CHUNKS):
        rows = lambda j: pl.ds(pl.multiple_of((j * SY + o) * piece, piece), n * piece)
        ring(f"xp_{k}", blk(x), rows(y), row_p, y)
        ring(f"xm_{k}", blk(x), rows(y), row_m, y)
        ring(f"xpf_{k}", ent(2 * xm), rows(y), row_p, y)
        ring(f"xmf_{k}", ent(2 * xp + 1), rows(y), row_m, y)
        for tag, j in (("yp", yp), ("ym", ym)):
            for i, b in enumerate((xm, xp, x2)):
                ring(f"{tag}{i + 1}_{k}", blk(b), rows(y), row, j)
        ring(f"ypf1_{k}", blk(xm), rows(ym), row, yp)
        ring(f"ypf3_{k}", ent(2 * x2), rows(ym), row, yp)
        ring(f"ymf2_{k}", blk(xp), rows(yp), row, ym)
        ring(f"ymf3_{k}", ent(2 * x2 + 1), rows(yp), row, ym)
    for k, (o, n) in enumerate(SX_CHUNKS):
        rows = pl.ds((NY * SY + o) * piece, n * piece)
        ring(f"sp_{k}", blk(x), rows, row_p, y)
        ring(f"sm_{k}", blk(x), rows, row_m, y)
        ring(f"spf_{k}", ent(2 * xm), rows, row_p, y)
        ring(f"smf_{k}", ent(2 * xp + 1), rows, row_m, y)

    regions = [(y * SY * piece, SY * piece), (NY * SY * piece, SX * piece)]
    regions += [(lax.rem(y + d, NY) * SY * piece, SY * piece) for d in range(1, NY)]
    local = []
    for s, (start, n) in enumerate(regions):
        start = pl.multiple_of(start, piece) if s != 1 else start
        there = xb.at[row, pl.ds(start, n)]
        local.append(pltpu.make_async_copy(x_ref.at[pl.ds(c * half + start, n)], there, loc.at[s]))
        define(f"d_{s}", x_ref.at[pl.ds((1 - c) * half + start, n)], there, partner, y)
    for d in range(1, n_ent):
        define(f"g_{d}", g_ref, gb.at[row], lax.rem(row + d, n_ent), y)
    define("wg", wg_ref, wgb.at[c], partner, y)
    define("wu", wu_ref, wub.at[c], partner, y)
    local.append(pltpu.make_async_copy(g_ref, gb.at[row], loc.at[NY + 1]))
    local.append(pltpu.make_async_copy(wg_ref, wgb.at[c], loc.at[NY + 2]))
    local.append(pltpu.make_async_copy(wu_ref, wub.at[c], loc.at[NY + 3]))
    for cp in local:
        cp.start()

    greet([(lax.rem(row + d, n_ent), y) for d in range(1, n_ent)] + [(row, yp), (row, ym)])

    for n in [f"d_{s}" for s in range(NY + 1)] + [f"g_{d}" for d in range(1, n_ent)] + ["wg", "wu"]:
        copies[n].start()

    def act(steps):
        for what, names in steps:
            if what == "rest":
                for s in range(1, NY + 1):
                    local[s].wait()
                    copies[f"d_{s}"].wait_recv()
            for n in names:
                if what == "s":
                    copies[n].start()
                elif what == "w":
                    copies[n].wait_recv()

    plan = k1_plan()
    local[0].wait()
    copies["d_0"].wait_recv()
    act(plan[-1])
    for cp in local[NY + 1 :]:
        cp.wait()
    for n in [f"g_{d}" for d in range(1, n_ent)] + ["wg", "wu"]:
        copies[n].wait_recv()

    base = {"s": y * SY, "m": ym * SY, "p": yp * SY, "o": y2 * SY, "x": NY * SY}
    per_tile = len(K1_TILES[0])

    def tile(s, _):
        for k in sorted(plan):
            if k >= 0:
                pl.when(s == k)(functools.partial(act, plan[k]))
        starts = []
        for i in range(per_tile):
            at = base[K1_TILES[0][i][0]] + K1_TILES[0][i][1]
            for k in range(1, len(K1_TILES)):
                kind, j = K1_TILES[k][i]
                at = jnp.where(s == k, base[kind] + j, at)
            starts.append(at * piece)

        for i, at in enumerate(starts):

            def sixteen(g, _, at=at, i=i):
                r = pl.multiple_of(at + g * 16, 16)
                d = pl.multiple_of(i * piece + g * 16, 16)

                def store(e, v):
                    nt[pl.ds(d, 16), e * width : (e + 1) * width] = v

                norm_rows(lambda e: xb[e, pl.ds(r, 16), :], gb, 0, store, n_ent, width)
                return 0

            lax.fori_loop(0, piece // 16, sixteen, 0)

        step = min(256, ff)
        for h in range(2):
            for col in range(0, ff, step):
                gate = jnp.dot(nt[...], wgb[h, :, col : col + step], preferred_element_type=F32)
                up = jnp.dot(nt[...], wub[h, :, col : col + step], preferred_element_type=F32)
                act_val = (gate * lax.logistic(gate) * up).astype(BF16)
                for i, at in enumerate(starts):
                    r = pl.multiple_of(at, 16)
                    a_ref[pl.ds(r, piece), h * ff + col : h * ff + col + step] = act_val[i * piece : (i + 1) * piece]
        return 0

    lax.fori_loop(0, len(K1_TILES), tile, 0)

    def keep(j, _):
        r = pl.multiple_of(j * NY * piece + y * piece, 16)
        for h in range(2):
            xres_ref[h, j] = xb[2 * x + h, pl.ds(r, piece), :]
        return 0

    lax.fori_loop(0, PIECES // NY, keep, 0)
    gout_ref[...] = gb[...]
    for n in ids:
        copies[n].wait_send()


AP, AM, APF, AMF, S1L, S1R, FL, FR, GL, GR = range(10)
QP, QM, QPF, QMF, QD0, QD1, QD2, QD3A, QD3B, WD = range(10)
RP, RM = 0, 2
RPF, RMF, RD = 4, 5, 6


def k2(
    a_ref, wd_ref, xres_ref, wq_ref, resid_ref, xn_ref, wqa_ref,
    aall, wdb, pbuf, r1, rf, send, recv, qsend, qrecv, rsend, rrecv, loc, rloc,
):
    x, c, row, y = place()
    xp, xm, _ = around(x, NX)
    yp, ym, y2 = around(y, NY)
    n_tiles = PIECES // NY
    piece, width = pbuf.shape[3], pbuf.shape[4]
    rows_n = NY * piece
    ffc = a_ref.shape[1]
    row_p, row_m, partner = 2 * xp + c, 2 * xm + c, 2 * x + 1 - c

    def cols(i):
        return pl.ds(pl.multiple_of(i * ffc, 128), ffc)

    first = pltpu.make_async_copy(a_ref.at[pl.ds(0, 2 * rows_n)], aall.at[pl.ds(0, 2 * rows_n), cols(x)], loc.at[0])
    rest_n = a_ref.shape[0] - 2 * rows_n
    rest = pltpu.make_async_copy(
        a_ref.at[pl.ds(2 * rows_n, rest_n)], aall.at[pl.ds(2 * rows_n, rest_n), cols(x)], loc.at[1]
    )
    wd_own = pltpu.make_async_copy(wd_ref, wdb.at[c], loc.at[2])
    first.start()
    wd_own.start()
    rest.start()

    greet([(row_p, y), (row_m, y), (partner, y), (row, yp), (row, ym), (partner, yp), (partner, ym)])

    def ring(kind, j, src, dst, to_row, to_y):
        return to(src, dst, send.at[kind, j], recv.at[kind, j], to_row, to_y)

    def own(j):
        ref = aall.at[pl.ds(pl.multiple_of(j * rows_n, 16), rows_n), cols(x)]
        return ring(AP, j, ref, ref, row_p, y), ring(AM, j, ref, ref, row_m, y)

    def onward(j):
        h = rows_n // 2
        up = aall.at[pl.ds(pl.multiple_of(j * rows_n, 16), h), cols(xm)]
        down = aall.at[pl.ds(pl.multiple_of(j * rows_n + h, 16), h), cols(xp)]
        return ring(APF, j, up, up, row_p, y), ring(AMF, j, down, down, row_m, y)

    def early(j):
        return (
            ring(S1L, j, pbuf.at[j, 0, y2], r1.at[j, 0], row, yp),
            ring(S1R, j, pbuf.at[j, 1, y2], r1.at[j, 1], row, ym),
            ring(FR, j, pbuf.at[j, 1, yp], rf.at[j, 1], row, yp),
            ring(GL, j, pbuf.at[j, 0, ym], rf.at[j, 2], row, ym),
        )

    def late(j):
        return (
            ring(FL, j, pbuf.at[j, 0, yp], rf.at[j, 0], row, yp),
            ring(GR, j, pbuf.at[j, 1, ym], rf.at[j, 3], row, ym),
        )

    def q(i, src, dst, to_row, to_y):
        return to(src, dst, qsend.at[i], qrecv.at[i], to_row, to_y)

    qn = wq_ref.shape[0]
    cut = (qn // 2 + 15) // 16 * 16
    lo, hi = pl.ds(0, cut), pl.ds(cut, qn - cut)
    mine, b_m, b_p, b_2 = 2 * y + c, 2 * ym + c, 2 * yp + c, 2 * y2 + c
    qs = {
        QP: q(QP, wq_ref, wqa_ref.at[mine], row, yp),
        QM: q(QM, wq_ref, wqa_ref.at[mine], row, ym),
        QPF: q(QPF, wqa_ref.at[b_m, lo], wqa_ref.at[b_m, lo], row, yp),
        QMF: q(QMF, wqa_ref.at[b_p, hi], wqa_ref.at[b_p, hi], row, ym),
        QD0: q(QD0, wq_ref, wqa_ref.at[mine], partner, y),
        QD1: q(QD1, wqa_ref.at[b_m], wqa_ref.at[b_m], partner, y),
        QD2: q(QD2, wqa_ref.at[b_p], wqa_ref.at[b_p], partner, y),
        QD3A: q(QD3A, wqa_ref.at[b_2, lo], wqa_ref.at[b_2, lo], partner, y),
        QD3B: q(QD3B, wqa_ref.at[b_2, hi], wqa_ref.at[b_2, hi], partner, y),
        WD: q(WD, wd_ref, wdb.at[c], partner, y),
    }

    def out(jj):
        two = pl.ds(2 * jj, 2)
        there = resid_ref.at[c, two, y]
        sends = []
        for h in range(2):
            src = xn_ref.at[h, two]
            sends.append(to(src, there, rsend.at[RP + h, jj], rrecv.at[RP + c, jj], 2 * x + h, yp))
            sends.append(to(src, there, rsend.at[RM + h, jj], rrecv.at[RM + c, jj], 2 * x + h, ym))
        sends.append(to(xn_ref.at[1 - c, two], there, rsend.at[RD, jj], rrecv.at[RD, jj], partner, y))
        return sends

    def out_own(jj):
        two = pl.ds(2 * jj, 2)
        return pltpu.make_async_copy(xn_ref.at[c, two], resid_ref.at[c, two, y], rloc.at[jj])

    def arrived(jj):
        two = pl.ds(2 * jj, 2)
        return [
            to(xn_ref.at[0, two], resid_ref.at[0, two, y], rsend.at[i, jj], rrecv.at[i, jj], row, yp) for i in range(4)
        ]

    def relay(jj):
        two = pl.ds(2 * jj, 2)
        up, down = resid_ref.at[0, two, ym], resid_ref.at[1, two, yp]
        return (
            to(up, up, rsend.at[RPF, jj], rrecv.at[RPF, jj], row, yp),
            to(down, down, rsend.at[RMF, jj], rrecv.at[RMF, jj], row, ym),
        )

    def start(cps):
        for cp in cps:
            cp.start()

    def got(cps):
        for cp in cps:
            cp.wait_recv()

    def step2(j):
        got(early(j)[:2])
        for r in range(0, piece, 16):
            s = pl.ds(r, 16)
            pbuf[j, 0, yp, s, :] = pbuf[j, 0, yp, s, :] + r1[j, 0, s, :]
            pbuf[j, 1, ym, s, :] = pbuf[j, 1, ym, s, :] + r1[j, 1, s, :]
        start(late(j))

    def final(j):
        got(early(j)[2:] + late(j))
        for h in range(2):
            for r in range(0, piece, 16):
                s = pl.ds(r, 16)
                total = pbuf[j, h, y, s, :] + rf[j, h, s, :] + rf[j, 2 + h, s, :]
                xn_ref[h, j, s, :] = (xres_ref[h, j, s, :].astype(F32) + total).astype(BF16)

    def relay_now(jj):
        got(arrived(jj))
        start(relay(jj))

    first.wait()
    start(own(0))
    qs[WD].start()
    start(own(1))
    start([qs[QP], qs[QM], qs[QD0]])
    rest.wait()
    wd_own.wait()
    qs[WD].wait_recv()

    step = min(256, width)

    def tile(j, _):
        @pl.when(j < n_tiles)
        def _():
            got(own(j))
            start(onward(j))

        @pl.when(j + 2 < n_tiles)
        def _():
            start(own(j + 2))

        @pl.when(j == 2)
        def _():
            got([qs[QP], qs[QM]])
            start([qs[QPF], qs[QMF], qs[QD1], qs[QD2]])

        @pl.when(j == 5)
        def _():
            got([qs[QPF], qs[QMF]])
            start([qs[QD3A], qs[QD3B]])

        @pl.when((j >= 1) & (j <= n_tiles))
        def _():
            step2(j - 1)

        @pl.when(j >= 2)
        def _():
            final(j - 2)

        @pl.when((j >= 3) & (lax.rem(j, 2) == 1))
        def _():
            jj = lax.div(j - 3, 2)
            start(out(jj))
            out_own(jj).start()

        @pl.when((j >= 5) & (lax.rem(j, 2) == 1))
        def _():
            relay_now(lax.div(j - 5, 2))

        @pl.when(j < n_tiles)
        def _():
            got(onward(j))
            lhs = pl.ds(pl.multiple_of(j * rows_n, 16), rows_n)
            for h in range(2):
                for col in range(0, width, step):
                    part = jnp.dot(aall[lhs, :], wdb[h, :, col : col + step], preferred_element_type=F32)
                    for i in range(NY):
                        pbuf[j, h, i, :, col : col + step] = part[i * piece : (i + 1) * piece]
            start(early(j))

        return 0

    lax.fori_loop(0, n_tiles + 2, tile, 0)
    relay_now(n_tiles // 2 - 1)

    got([qs[i] for i in (QD0, QD1, QD2, QD3A, QD3B)])

    def settle(j, _):
        for cp in own(j) + onward(j) + early(j) + late(j):
            cp.wait_send()
        return 0

    lax.fori_loop(0, n_tiles, settle, 0)

    def settle_out(jj, _):
        for cp in out(jj) + list(relay(jj)):
            cp.wait_send()
        got([out(jj)[-1]] + list(relay(jj)))
        out_own(jj).wait()
        return 0

    lax.fori_loop(0, n_tiles // 2, settle_out, 0)
    for i in qs:
        qs[i].wait_send()


def k3(xn_ref, gb_ref, wq_ref, wqa_ref, out_ref, xg, wqb, nt, ob, send, recv, osend, orecv, loc, oloc):
    x, c, row, y = place()
    xp, xm, _ = around(x, NX)
    n_ent = 2 * NX
    n_chunks = xg.shape[1] // 2
    piece, width = xg.shape[2], xg.shape[3]
    row_p, row_m, partner = 2 * xp + c, 2 * xm + c, 2 * x + 1 - c
    mine = 2 * y + c

    own = pltpu.make_async_copy(xn_ref, xg.at[pl.ds(2 * x, 2)], loc.at[0])
    own.start()
    loads = [pltpu.make_async_copy(wq_ref, wqb.at[mine], loc.at[1])]
    for d in range(1, 2 * NY):
        b = lax.rem(mine + d, 2 * NY)
        loads.append(pltpu.make_async_copy(wqa_ref.at[b], wqb.at[b], loc.at[1 + d]))
    for cp in loads:
        cp.start()

    column = [(2 * x + h, lax.rem(y + d, NY)) for d in range(1, NY) for h in range(2)]
    greet([(row_p, y), (row_m, y), (partner, y)] + column)

    def ring(kind, q, ents, to_row):
        ref = xg.at[ents, pl.ds(2 * q, 2)]
        return to(ref, ref, send.at[kind, q], recv.at[kind, q], to_row, y)

    def mains(q):
        return ring(0, q, pl.ds(2 * x, 2), row_p), ring(1, q, pl.ds(2 * x, 2), row_m)

    def onward(q):
        return ring(2, q, pl.ds(2 * xm, 1), row_p), ring(3, q, pl.ds(2 * xp + 1, 1), row_m)

    def result(q, d, f):
        h = c if f == 0 else 1 - c
        i = 2 * d + f
        src, dst = ob.at[q, i], out_ref.at[c, pl.ds(2 * q, 2), y]
        if i == 0:
            return pltpu.make_async_copy(src, dst, oloc.at[q])
        return to(src, dst, osend.at[q, i], orecv.at[q, i], 2 * x + h, lax.rem(y + d, NY))

    own.wait()
    for q in range(n_chunks):
        for cp in mains(q):
            cp.start()
        if q == 0:
            for cp in mains(q):
                cp.wait_recv()
            for cp in onward(q):
                cp.start()
    for cp in loads:
        cp.wait()

    def chunk(q, _):
        for cp in onward(q):
            cp.wait_recv()

        @pl.when(q + 1 < n_chunks)
        def _():
            for cp in mains(q + 1):
                cp.wait_recv()
            for cp in onward(q + 1):
                cp.start()

        for t in range(2):

            def sixteen(g, _, t=t):
                r = pl.multiple_of(g * 16, 16)
                d = pl.multiple_of(t * piece + g * 16, 16)

                def store(e, v):
                    nt[pl.ds(d, 16), e * width : (e + 1) * width] = v

                norm_rows(lambda e: xg[e, 2 * q + t, pl.ds(r, 16), :], gb_ref, 1, store, n_ent, width)
                return 0

            lax.fori_loop(0, piece // 16, sixteen, 0)

        for d in (2, 1, 3, 0):
            for f in range(2):
                h = c if f == 0 else 1 - c
                b = 2 * lax.rem(y + d, NY) + h
                part = lax.dot_general(nt[...], wqb[b], (((1,), (1,)), ((), ())), preferred_element_type=F32)
                part = part.astype(BF16)
                for t in range(2):
                    ob[q, 2 * d + f, t] = part[t * piece : (t + 1) * piece]
                result(q, d, f).start()
        return 0

    lax.fori_loop(0, n_chunks, chunk, 0)

    def settle(q, _):
        for cp in mains(q) + onward(q):
            cp.wait_send()
        for d in range(NY):
            for f in range(2):
                result(q, d, f).wait()
        return 0

    lax.fori_loop(0, n_chunks, settle, 0)


def solution(mesh):
    assert mesh.shape["row"] == 2 * NX and mesh.shape["col"] == NY
    tok_spec, gain_spec = P("data", "row"), P("row")
    wide_spec, down_spec, qkv_spec = P(None, ("col", "row")), P("col", "row"), P("data", ("col", "row"))

    def params(i):
        return pltpu.CompilerParams(collective_id=i, has_side_effects=True, vmem_limit_bytes=LIMIT)

    def per_device(residual, gain_mlp, gain_attn, w_gate, w_up, w_down, w_qkv):
        tokens, width = residual.shape
        hidden, ff = w_gate.shape
        qn = w_qkv.shape[1]
        half = tokens // 2
        piece = half // PIECES
        tiles = PIECES // NY
        n_ent = 2 * NX
        gains = jnp.concatenate([gain_mlp[None], gain_attn[None], jnp.zeros((6, width), F32)])
        wq = w_qkv.T
        n1 = len(k1_names())
        act, xres, gb = pl.pallas_call(
            k1,
            name="gather_mlp_in",
            out_shape=[
                jax.ShapeDtypeStruct((half, 2 * ff), BF16),
                jax.ShapeDtypeStruct((2, tiles, piece, width), BF16),
                jax.ShapeDtypeStruct((n_ent, 8, width), F32),
            ],
            in_specs=[ANY] * 4,
            out_specs=[VMEM] * 3,
            scratch_shapes=[
                pltpu.VMEM((n_ent, half, width), BF16),
                pltpu.VMEM((2, hidden, ff), BF16),
                pltpu.VMEM((2, hidden, ff), BF16),
                pltpu.VMEM((len(K1_TILES[0]) * piece, hidden), BF16),
                pltpu.VMEM((n_ent, 8, width), F32),
                DMA((n1,)),
                DMA((n1,)),
                DMA((NY + 4,)),
            ],
            compiler_params=params(1),
        )(residual, gains, w_gate, w_up)
        resid, xn, wqa = pl.pallas_call(
            k2,
            name="gather_mlp_out",
            out_shape=[
                jax.ShapeDtypeStruct((2, tiles, NY, piece, width), BF16),
                jax.ShapeDtypeStruct((2, tiles, piece, width), BF16),
                jax.ShapeDtypeStruct((2 * NY, qn, hidden), BF16),
            ],
            in_specs=[ANY, ANY, VMEM, ANY],
            out_specs=[ANY, VMEM, ANY],
            scratch_shapes=[
                pltpu.VMEM((half, n_ent * ff), BF16),
                pltpu.VMEM((2, n_ent * ff, width), BF16),
                pltpu.VMEM((tiles, 2, NY, piece, width), F32),
                pltpu.VMEM((tiles, 2, piece, width), F32),
                pltpu.VMEM((tiles, 4, piece, width), F32),
                DMA((10, tiles)),
                DMA((10, tiles)),
                DMA((10,)),
                DMA((10,)),
                DMA((7, tiles // 2)),
                DMA((7, tiles // 2)),
                DMA((3,)),
                DMA((tiles // 2,)),
            ],
            compiler_params=params(2),
        )(act, w_down, xres, wq)
        (qkv,) = pl.pallas_call(
            k3,
            name="gather_qkv",
            out_shape=[jax.ShapeDtypeStruct((2, tiles, NY, piece, qn), BF16)],
            in_specs=[ANY, VMEM, ANY, ANY],
            out_specs=[ANY],
            scratch_shapes=[
                pltpu.VMEM((n_ent, tiles, piece, width), BF16),
                pltpu.VMEM((2 * NY, qn, hidden), BF16),
                pltpu.VMEM((2 * piece, hidden), BF16),
                pltpu.VMEM((tiles // 2, 2 * NY, 2, piece, qn), BF16),
                DMA((4, tiles // 2)),
                DMA((4, tiles // 2)),
                DMA((tiles // 2, 2 * NY)),
                DMA((tiles // 2, 2 * NY)),
                DMA((1 + 2 * NY,)),
                DMA((tiles // 2,)),
            ],
            compiler_params=params(3),
        )(xn, gb, wq, wqa)
        return resid.reshape(tokens, width), qkv.reshape(tokens, qn)

    return jax.shard_map(
        per_device,
        mesh=mesh,
        in_specs=(tok_spec, gain_spec, gain_spec, wide_spec, wide_spec, down_spec, wide_spec),
        out_specs=(tok_spec, qkv_spec),
        check_vma=False,
    )
```

time: 794 us -> 344 us (0.43)
  waiting for transfers between devices: 623 us -> 0 us
  Pallas kernels: 0 us -> 333 us
  matrix products: 90.3 us -> 0 us
  blocking collectives: 46.7 us -> 0 us
  other arithmetic: 19.4 us -> 1.37 us
  between operations: 13.8 us -> 0.66 us
  local copies, waits for them, and re-layouts: 0.02 us -> 8.28 us
    all_gather x3 -> x0, waiting for transfers between devices: 468 us -> none  [the longest x1 158 us: per_device(): normed_full = lax.all_gather(normed, 'row', axis=1, tiled=True)]
    pallas_call x0 -> x3, Pallas kernels: none -> 333 us  [the longest x1 181 us: per_device(): pl.pallas_call(k2, name='gather_mlp_out', out_shape=[jax.ShapeDtypeStruct...]
    psum x1 -> x0, waiting for transfers between devices: 155 us -> none  [per_device(): down_sum = lax.psum(down_part, 'col')]
    dot_general x4 -> x0, matrix products: 90.3 us -> none  [the longest x1 24.9 us: per_device(): down_part = jnp.dot(act_block, w_down, preferred_element_type=jnp.float32)]
    psum x2 -> x0, blocking collectives: 46.7 us -> none  [shard_norm(): sq_total = lax.psum(sq_part, 'row')]
    reduce_sum x2 -> x0, other arithmetic: 11 us -> none  [shard_norm(): sq_part = jnp.sum(shard_f * shard_f, axis=1, keepdims=True)]
    convert_element_type x2 -> x0, other arithmetic: 8.33 us -> none  [shard_norm(): return (shard_f * row_scale * gain).astype(jnp.bfloat16)]
    unnamed x6 -> x2, local copies, waits for them, and re-layouts: 0.02 us -> 8.2 us
  transfers between devices with their start and end apart: 4 -> 0, of which waited for: 4 -> 0; matrix products, arithmetic and copies ran while one was open for 0% -> 0% of each run, Pallas kernels for 0% -> 0%
where the time goes in v1:
time: 344 us; the launch traced here: 343 us
  Pallas kernels  333 us (97%)
  local copies, waits for them, and re-layouts  8.28 us (2%)
    pallas_call x1, Pallas kernels, per_device(): pl.pallas_call(k2, name='gather_mlp_out', out_shape=[jax.ShapeDtypeStruct...  181 us
    pallas_call x1, Pallas kernels, per_device(): pl.pallas_call(k1, name='gather_mlp_in', out_shape=[jax.ShapeDtypeStruct(...  94.2 us
    pallas_call x1, Pallas kernels, per_device(): pl.pallas_call(k3, name='gather_qkv', out_shape=[jax.ShapeDtypeStruct((2,...  58.4 us
    unnamed x2, local copies, waits for them, and re-layouts  8.2 us

profile of v1, /device:TPU:97, one launch (start us, length us, event | category | flops | bytes accessed | tf_op | source)
XLA Modules:
  0.0 343.4 jit_solution(16809495499140171318)
XLA Ops:
  0.6 0.1 pad.2.clone
  0.7 1.4 maximum_maximum_fusion.g_ref
  2.1 94.2 %gather_mlp_in.1 = (bf16[2048,1024]{1,0:T(8,128)(2,1)}, bf16[2,8,64,512]{3,2,1,0:T(8,128)(2,1)}, f32[8,8,512]{2,1,0:T(8,128)}) custom-call(bf16[4096,512]{1,0:T(8,128)(2,1)} %x_ref.1, f32[8,512]{1,0:T(8,128)} %maximum_maximum_fusion.g_ref, bf16[4096,512]{1,0:T(8,128)(2,1)} %wg_ref.1, bf16[4096,512]{1,0:T(8,128)(2,1)} %wu_ref.1), custom_call_target="tpu_custom_call" | custom-call | tf_op jit(solution)/shard_map/gather_mlp_in/pallas_call | solution.py:620
  96.2 180.6 %gather_mlp_out.1 = (bf16[2,8,4,64,512]{4,3,2,1,0:T(8,128)(2,1)}, bf16[2,8,64,512]{3,2,1,0:T(8,128)(2,1)}, bf16[8,144,4096]{2,1,0:T(8,128)(2,1)}) custom-call(bf16[2048,1024]{1,0:T(8,128)(2,1)} %get-tuple-element.8.a_ref, bf16[4096,512]{1,0:T(8,128)(2,1)} %wd_ref.1, bf16[2,8,64,512]{3,2,1,0:T(8,128)(2,1)} %get-tuple-element.9.xres_ref, bf16[144,4096]{1,0:T(8,128)(2,1)} %bitcast.6), custom_call_target="tpu_custom_call" | custom-call | tf_op jit(solution)/shard_map/gather_mlp_out/pallas_call | solution.py:642
  276.8 58.4 %gather_qkv.1 = bf16[2,8,4,64,144]{4,3,2,1,0:T(8,128)(2,1)} custom-call(bf16[2,8,64,512]{3,2,1,0:T(8,128)(2,1)} %get-tuple-element.11.xn_ref, f32[8,8,512]{2,1,0:T(8,128)} %get-tuple-element.12.gb_ref, bf16[144,4096]{1,0:T(8,128)(2,1)} %bitcast.7, bf16[8,144,4096]{2,1,0:T(8,128)(2,1)} %get-tuple-element.13.wqa_ref), custom_call_target="tpu_custom_call" | custom-call | tf_op jit(solution)/shard_map/gather_qkv/pallas_call | solution.py:669
  335.2 3.7 %copy.9 = bf16[4096,144]{0,1:T(8,128)(2,1)} copy(bf16[4096,144]{1,0:T(8,128)(2,1)} %bitcast.5) | data formatting | bytes 2359296
  339.0 4.5 %copy.11 = bf16[4096,512]{1,0:T(8,128)(2,1)} copy(bf16[4096,512]{1,0:T(8,128)(2,1)} %bitcast.8) | data formatting | bytes 8388608
  (1 shorter events, 0.0 us)

commit v2 on v0

v2 whole, which is shorter than its diff:
```python
import functools

import jax
import jax.numpy as jnp
from jax import lax
from jax.experimental import pallas as pl
from jax.experimental.pallas import tpu as pltpu
from jax.sharding import PartitionSpec as P

NORM_EPS = 1e-6
MESH = pl.DeviceIdType.MESH
BF16 = jnp.bfloat16
F32 = jnp.float32
ANY = pl.BlockSpec(memory_space=pl.ANY)
VMEM = pl.BlockSpec(memory_space=pltpu.VMEM)
DMA = pltpu.SemaphoreType.DMA
LIMIT = 64 * 1024 * 1024 - 128 * 1024

NX, NY = 4, 4
PAIRS = 16
SY = 3
SX = PAIRS - NY * SY
EARLY = 2
TILES = PAIRS // 2
SHIFT = TILES - EARLY
CHUNKS = TILES // 2


def place():
    row, y = lax.axis_index("row"), lax.axis_index("col")
    return lax.div(row, 2), lax.rem(row, 2), row, y


def around(i, n):
    return lax.rem(i + 1, n), lax.rem(i + n - 1, n), lax.rem(i + 2, n)


def greet(peers):
    barrier = pltpu.get_barrier_semaphore()
    for row, y in peers:
        pl.semaphore_signal(barrier, inc=1, device_id={"row": row, "col": y}, device_id_type=MESH)
    pl.semaphore_wait(barrier, len(peers))


def to(src, dst, send, recv, row, y):
    return pltpu.make_async_remote_copy(src, dst, send, recv, device_id={"row": row, "col": y}, device_id_type=MESH)


def start(copies):
    for cp in copies:
        cp.start()


def got(copies):
    for cp in copies:
        cp.wait_recv()


def norm_rows(load, gains, which, store, n_ent, width):
    acc = None
    for e in range(n_ent):
        v = load(e).astype(F32)
        acc = v * v if acc is None else acc + v * v
    scale = lax.rsqrt(jnp.sum(acc, axis=1, keepdims=True) / (n_ent * width) + NORM_EPS)
    for e in range(n_ent):
        store(e, (load(e).astype(F32) * scale * gains[e, which : which + 1, :]).astype(BF16))


GROUPS = {
    "xp": ("xp", "xm"),
    "xf": ("xpf", "xmf"),
    "ya": ("yp1", "yp2", "ym1", "ym2"),
    "yb": ("yp3", "ym3"),
    "yf": ("ypf1", "ypf3", "ymf2", "ymf3"),
    "s": ("sp", "sm"),
    "sf": ("spf", "smf"),
    "a": ("ap", "am"),
    "af": ("apf", "amf"),
}
COUNTS = {"xp": SY, "xf": SY, "ya": SY, "yb": SY, "yf": SY, "s": SX, "sf": SX, "a": EARLY, "af": EARLY}

K1_TILES = ("s0", "m0", "s1", "s2", "p0", "x0", "o0", "x1", "m1", "x2", "x3", "p1", "m2", "p2", "o1", "o2")
K1_PLAN = (
    ("s", "xp0", "xp1", "xp2", "w", "xp0", "s", "xf0", "ya0", "s0", "w", "xp1", "s", "xf1", "w", "xp2", "s", "xf2", "w", "xf0", "s", "yb0", "ya1"),
    ("s", "s1", "w", "s0", "s", "sf0", "w", "ya0", "yb0", "s", "yf0"),
    ("w", "xf1", "s", "yb1", "ya2", "w", "xf2", "s", "yb2", "s2"),
    (),
    ("w", "s1", "s", "sf1"),
    ("s", "s3", "w", "sf0"),
    ("w", "s2", "s", "sf2", "w", "yf0"),
    ("w", "sf1"),
    ("w", "ya1", "yb1", "s", "yf1", "w", "s3", "s", "sf3", "a0"),
    ("w", "sf2"),
    ("w", "sf3"),
    ("s", "a1"),
    ("w", "ya2", "yb2", "s", "yf2"),
    ("w", "a0", "s", "af0"),
    ("w", "yf1"),
    ("w", "a1", "s", "af1", "w", "yf2"),
    ("w", "af0", "af1"),
)


def k1_steps(tokens):
    steps, what = [], None
    for token in tokens:
        if token in ("s", "w"):
            what = token
        else:
            steps.append((what, token))
    return steps


def k1_names():
    names = []
    for group, parts in GROUPS.items():
        for k in range(COUNTS[group]):
            for part in parts:
                names += [f"{part}{k}a", f"{part}{k}b"] if group == "xp" and k == 0 else [f"{part}{k}"]
    names += [f"d{s}" for s in range(NY + 1)]
    names += [f"g{d}" for d in range(1, 2 * NX)]
    return names + ["wg", "wu"]


def k1(x_ref, g_ref, wg_ref, wu_ref, a_ref, xres_ref, gout_ref, ag_ref, xb, wgb, wub, nt, gb, send, recv, loc):
    x, c, row, y = place()
    xp, xm, x2 = around(x, NX)
    yp, ym, y2 = around(y, NY)
    n_ent = 2 * NX
    piece, width, ff = xb.shape[3], xb.shape[4], wgb.shape[2]
    ids = {n: i for i, n in enumerate(k1_names())}
    partner = 2 * x + 1 - c
    row_p, row_m = 2 * xp + c, 2 * xm + c
    copies = {}

    def define(name, src, dst, to_row, to_y):
        i = ids[name]
        copies[name] = to(src, dst, send.at[i], recv.at[i], to_row, to_y)

    def ring(name, ents, where, to_row, to_y):
        ref = xb.at[(ents, *where)]
        define(name, ref, ref, to_row, to_y)

    blk = lambda i: pl.ds(2 * i, 2)
    ent = lambda i: pl.ds(i, 1)
    for k in range(SY):
        rows = lambda j: (pl.ds(j * SY + k, 1),)
        for part, j in (("xp", row_p), ("xm", row_m)):
            if k == 0:
                ring(f"{part}0a", ent(row), rows(y), j, y)
                ring(f"{part}0b", ent(partner), rows(y), j, y)
            else:
                ring(f"{part}{k}", blk(x), rows(y), j, y)
        ring(f"xpf{k}", ent(2 * xm), rows(y), row_p, y)
        ring(f"xmf{k}", ent(2 * xp + 1), rows(y), row_m, y)
        for tag, j in (("yp", yp), ("ym", ym)):
            for i, b in enumerate((xm, xp, x2)):
                ring(f"{tag}{i + 1}{k}", blk(b), rows(y), row, j)
        ring(f"ypf1{k}", blk(xm), rows(ym), row, yp)
        ring(f"ypf3{k}", ent(2 * x2), rows(ym), row, yp)
        ring(f"ymf2{k}", blk(xp), rows(yp), row, ym)
        ring(f"ymf3{k}", ent(2 * x2 + 1), rows(yp), row, ym)
    for k in range(SX):
        rows = (pl.ds(NY * SY + k % 2 * 2, 2), k // 2)
        ring(f"sp{k}", blk(x), rows, row_p, y)
        ring(f"sm{k}", blk(x), rows, row_m, y)
        ring(f"spf{k}", ent(2 * xm), rows, row_p, y)
        ring(f"smf{k}", ent(2 * xp + 1), rows, row_m, y)
    n_tile = NY * piece
    for k in range(EARLY):
        src = a_ref.at[pl.ds((SHIFT + k) * n_tile, n_tile)]
        there = ag_ref.at[x, pl.ds(k * n_tile, n_tile)]
        up = ag_ref.at[xm, pl.ds(k * n_tile, n_tile // 2)]
        down = ag_ref.at[xp, pl.ds(k * n_tile + n_tile // 2, n_tile // 2)]
        define(f"ap{k}", src, there, row_p, y)
        define(f"am{k}", src, there, row_m, y)
        define(f"apf{k}", up, up, row_p, y)
        define(f"amf{k}", down, down, row_m, y)

    regions = [(y * SY, SY), (NY * SY, SX)] + [(lax.rem(y + d, NY) * SY, SY) for d in range(1, NY)]
    local = []
    for s, (first, n) in enumerate(regions):
        there = xb.at[row, pl.ds(first, n)]
        local.append(pltpu.make_async_copy(x_ref.at[c, pl.ds(first, n)], there, loc.at[s]))
        define(f"d{s}", x_ref.at[1 - c, pl.ds(first, n)], there, partner, y)
    for d in range(1, n_ent):
        define(f"g{d}", g_ref, gb.at[row], lax.rem(row + d, n_ent), y)
    define("wg", wg_ref, wgb.at[c], partner, y)
    define("wu", wu_ref, wub.at[c], partner, y)
    local.append(pltpu.make_async_copy(g_ref, gb.at[row], loc.at[NY + 1]))
    local.append(pltpu.make_async_copy(wg_ref, wgb.at[c], loc.at[NY + 2]))
    local.append(pltpu.make_async_copy(wu_ref, wub.at[c], loc.at[NY + 3]))
    start(local)

    greet([(lax.rem(row + d, n_ent), y) for d in range(1, n_ent)] + [(row, yp), (row, ym)])

    copies["d0"].start()
    local[0].wait()
    start([copies["xp0a"], copies["xm0a"]])
    rest = [f"d{s}" for s in range(1, NY + 1)] + [f"g{d}" for d in range(1, n_ent)]
    start([copies[n] for n in rest + ["wg", "wu"]])
    got([copies["d0"]])
    start([copies["xp0b"], copies["xm0b"]])

    def act(tokens):
        for what, token in k1_steps(tokens):
            group, k = token[:-1], int(token[-1])
            if what == "s" and token == "s0":
                for s in range(1, NY + 1):
                    local[s].wait()
                    copies[f"d{s}"].wait_recv()
            for part in GROUPS[group]:
                for name in [f"{part}{k}a", f"{part}{k}b"] if token == "xp0" else [f"{part}{k}"]:
                    if what == "w":
                        copies[name].wait_recv()
                    elif token != "xp0":
                        copies[name].start()

    act(K1_PLAN[0])
    for cp in local[NY + 1 :]:
        cp.wait()
    got([copies[n] for n in [f"g{d}" for d in range(1, n_ent)] + ["wg", "wu"]])

    base = {"s": y * SY, "m": ym * SY, "p": yp * SY, "o": y2 * SY}

    def tile(s, _):
        for k in range(1, len(K1_TILES)):
            if K1_PLAN[k]:
                pl.when(s == k)(functools.partial(act, K1_PLAN[k]))
        pair, late, along = 0, 0, 0
        for k, name in enumerate(K1_TILES):
            i = int(name[1])
            where = (NY * SY + i % 2 * 2, i // 2, 1) if name[0] == "x" else (base[name[0]] + i, 0, 0)
            pair, late, along = (jnp.where(s == k, a, b) for a, b in zip(where, (pair, late, along)))
        pieces = [(pair, late), (pair + along, late + 1 - along)]

        for i, (p, t) in enumerate(pieces):

            def sixteen(g, _, p=p, t=t, i=i):
                r = pl.multiple_of(g * 16, 16)
                d = pl.multiple_of(i * piece + g * 16, 16)

                def store(e, v):
                    nt[pl.ds(d, 16), e * width : (e + 1) * width] = v

                norm_rows(lambda e: xb[e, p, t, pl.ds(r, 16), :], gb, 0, store, n_ent, width)
                return 0

            lax.fori_loop(0, piece // 16, sixteen, 0)

        step = min(256, ff)
        for h in range(2):
            for col in range(0, ff, step):
                gate = jnp.dot(nt[...], wgb[h, :, col : col + step], preferred_element_type=F32)
                up = jnp.dot(nt[...], wub[h, :, col : col + step], preferred_element_type=F32)
                act_val = (gate * lax.logistic(gate) * up).astype(BF16)
                for i, (p, t) in enumerate(pieces):
                    at = (p - lax.rem(p, NY)) * 2 + t * NY + lax.rem(p, NY)
                    r = pl.multiple_of(at * piece, 16)
                    a_ref[pl.ds(r, piece), h * ff + col : h * ff + col + step] = act_val[i * piece : (i + 1) * piece]
        return 0

    lax.fori_loop(0, len(K1_TILES), tile, 0)

    for q in range(CHUNKS):
        for t in range(2):
            for h in range(2):
                xres_ref[h, q, t] = xb[2 * x + h, NY * q + y, t]
    gout_ref[...] = gb[...]
    act(K1_PLAN[-1])
    for n in ids:
        copies[n].wait_send()


SEND = (5, 6, 6, 6, 6, 7, 9, 11)
PASS = (7, 8, 10, 9, 9, 8, 11, 11)
OUT = (3, 5, 8, 9)
RELAY = (5, 7, 10, 11)
QKV = (9, 11, 11, 11)
STEPS = 12
QKV_ORDER = tuple(sorted(range(CHUNKS), key=lambda n: (QKV[n], n)))

AP, AM, APF, AMF, S1L, S1R, FL, FR, GL, GR, XP, XM, XPF, XMF = range(14)
QPA, QPB, QMB, QMA, QPF, QMF, QD0, QD1, QD2, QD3A, QD3B, WD = range(12)
RP, RM, RPF, RMF, RD = 0, 2, 4, 5, 6


def k2(
    a_ref, ag_ref, wd_ref, xres_ref, gb_ref, wq_ref, resid_ref, out_ref,
    aall, wdb, pbuf, r1, rf, xg, wqb, nt, ob,
    send, recv, qsend, qrecv, rsend, rrecv, osend, orecv, loc, rloc, oloc,
):
    x, c, row, y = place()
    xp, xm, _ = around(x, NX)
    yp, ym, y2 = around(y, NY)
    n_ent = 2 * NX
    piece, width = pbuf.shape[3], pbuf.shape[4]
    rows_n = NY * piece
    ffc = a_ref.shape[1]
    qn = wq_ref.shape[0]
    row_p, row_m, partner = 2 * xp + c, 2 * xm + c, 2 * x + 1 - c

    def cols(i):
        return pl.ds(pl.multiple_of(i * ffc, 128), ffc)

    def at(i):
        return lax.rem(i + SHIFT, TILES)

    def chunk_of(n):
        return lax.rem(n + SHIFT // 2, CHUNKS)

    def rows(i, off=0, n=rows_n):
        return pl.ds(pl.multiple_of(at(i) * rows_n + off, 16), n)

    def wq_at(b, off=0, n=qn):
        return wqb.at[pl.ds(pl.multiple_of(b * qn + off, 16), n)]

    early_n = EARLY * rows_n
    cut = 2 * rows_n
    tail = pl.ds(SHIFT * rows_n, early_n)
    local = [
        pltpu.make_async_copy(a_ref.at[pl.ds(0, cut)], aall.at[pl.ds(0, cut), cols(x)], loc.at[0]),
        pltpu.make_async_copy(wd_ref, wdb.at[c], loc.at[1]),
        pltpu.make_async_copy(a_ref.at[pl.ds(cut, TILES * rows_n - cut)], aall.at[pl.ds(cut, TILES * rows_n - cut), cols(x)], loc.at[2]),
        pltpu.make_async_copy(wq_ref, wq_at(2 * y + c), loc.at[3]),
    ]
    for d in range(1, NX):
        other = lax.rem(x + d, NX)
        local.append(pltpu.make_async_copy(ag_ref.at[other], aall.at[tail, cols(other)], loc.at[3 + d]))
    start(local)

    column = [(2 * x + h, lax.rem(y + d, NY)) for d in range(1, NY) for h in range(2)]
    greet([(row_p, y), (row_m, y), (partner, y)] + column)

    def ring(kind, j, src, dst, to_row, to_y):
        return to(src, dst, send.at[kind, j], recv.at[kind, j], to_row, to_y)

    def own(i):
        ref = aall.at[rows(i), cols(x)]
        return ring(AP, i, ref, ref, row_p, y), ring(AM, i, ref, ref, row_m, y)

    def onward(i):
        h = rows_n // 2
        up, down = aall.at[rows(i, 0, h), cols(xm)], aall.at[rows(i, h, h), cols(xp)]
        return ring(APF, i, up, up, row_p, y), ring(AMF, i, down, down, row_m, y)

    def early(i):
        return (
            ring(S1L, i, pbuf.at[i, 0, y2], r1.at[i, 0], row, yp),
            ring(S1R, i, pbuf.at[i, 1, y2], r1.at[i, 1], row, ym),
            ring(FR, i, pbuf.at[i, 1, yp], rf.at[i, 1], row, yp),
            ring(GL, i, pbuf.at[i, 0, ym], rf.at[i, 2], row, ym),
        )

    def late(i):
        return (
            ring(FL, i, pbuf.at[i, 0, yp], rf.at[i, 0], row, yp),
            ring(GR, i, pbuf.at[i, 1, ym], rf.at[i, 3], row, ym),
        )

    def next_own(i):
        ref = xg.at[pl.ds(2 * x, 2), i]
        return ring(XP, i, ref, ref, row_p, y), ring(XM, i, ref, ref, row_m, y)

    def next_onward(i):
        up, down = xg.at[pl.ds(2 * xm, 1), i], xg.at[pl.ds(2 * xp + 1, 1), i]
        return ring(XPF, i, up, up, row_p, y), ring(XMF, i, down, down, row_m, y)

    def q(i, ref, to_row, to_y, src=None):
        return to(ref if src is None else src, ref, qsend.at[i], qrecv.at[i], to_row, to_y)

    n_a = (qn // 2 + 15) // 16 * 16
    n_b = qn - n_a
    mine, b_m, b_p, b_2 = 2 * y + c, 2 * ym + c, 2 * yp + c, 2 * y2 + c
    src_a, src_b = wq_ref.at[pl.ds(0, n_a)], wq_ref.at[pl.ds(n_a, n_b)]
    qs = {
        QPA: q(QPA, wq_at(mine, 0, n_a), row, yp, src_a),
        QPB: q(QPB, wq_at(mine, n_a, n_b), row, yp, src_b),
        QMB: q(QMB, wq_at(mine, n_a, n_b), row, ym, src_b),
        QMA: q(QMA, wq_at(mine, 0, n_a), row, ym, src_a),
        QPF: q(QPF, wq_at(b_m, 0, n_a), row, yp),
        QMF: q(QMF, wq_at(b_p, n_a, n_b), row, ym),
        QD0: q(QD0, wq_at(mine), partner, y, wq_ref),
        QD1: q(QD1, wq_at(b_m), partner, y),
        QD2: q(QD2, wq_at(b_p), partner, y),
        QD3A: q(QD3A, wq_at(b_2, 0, n_a), partner, y),
        QD3B: q(QD3B, wq_at(b_2, n_a, n_b), partner, y),
        WD: to(wd_ref, wdb.at[c], qsend.at[WD], qrecv.at[WD], partner, y),
    }

    def out(n):
        there = resid_ref.at[c, chunk_of(n), y]
        sends = []
        for h in range(2):
            src = xg.at[2 * x + h, pl.ds(2 * n, 2)]
            sends.append(to(src, there, rsend.at[RP + h, n], rrecv.at[RP + c, n], 2 * x + h, yp))
            sends.append(to(src, there, rsend.at[RM + h, n], rrecv.at[RM + c, n], 2 * x + h, ym))
        sends.append(to(xg.at[partner, pl.ds(2 * n, 2)], there, rsend.at[RD, n], rrecv.at[RD, n], partner, y))
        return sends

    def out_own(n):
        return pltpu.make_async_copy(xg.at[row, pl.ds(2 * n, 2)], resid_ref.at[c, chunk_of(n), y], rloc.at[n])

    def out_arrived(n):
        ref = resid_ref.at[0, chunk_of(n), y]
        return [to(xg.at[row, pl.ds(2 * n, 2)], ref, rsend.at[i, n], rrecv.at[i, n], row, yp) for i in range(4)]

    def relay(n):
        up, down = resid_ref.at[0, chunk_of(n), ym], resid_ref.at[1, chunk_of(n), yp]
        return (
            to(up, up, rsend.at[RPF, n], rrecv.at[RPF, n], row, yp),
            to(down, down, rsend.at[RMF, n], rrecv.at[RMF, n], row, ym),
        )

    def result(n, d, f):
        h = c if f == 0 else 1 - c
        to_y = lax.rem(y + d, NY)
        src = ob.at[n, 2 * to_y + h]
        first = (c * CHUNKS + chunk_of(n)) * NY + y
        dst = out_ref.at[:, pl.ds(pl.multiple_of(first * 2 * piece, 128), 2 * piece)]
        if d == 0 and f == 0:
            return pltpu.make_async_copy(src, dst, oloc.at[n])
        return to(src, dst, osend.at[n, 2 * d + f], orecv.at[n, 2 * d + f], 2 * x + h, to_y)

    def add_neighbour(i):
        got(early(i)[:2])
        for r in range(0, piece, 16):
            s = pl.ds(r, 16)
            pbuf[i, 0, yp, s, :] = pbuf[i, 0, yp, s, :] + r1[i, 0, s, :]
            pbuf[i, 1, ym, s, :] = pbuf[i, 1, ym, s, :] + r1[i, 1, s, :]
        start(late(i))

    def final(i):
        got(early(i)[2:] + late(i))
        for h in range(2):
            for r in range(0, piece, 16):
                s = pl.ds(r, 16)
                total = pbuf[i, h, y, s, :] + rf[i, h, s, :] + rf[i, 2 + h, s, :]
                held = xres_ref[h, lax.div(at(i), 2), lax.rem(i, 2), s, :].astype(F32)
                xg[2 * x + h, i, s, :] = (held + total).astype(BF16)

    def qkv(n):
        got(next_onward(2 * n) + next_onward(2 * n + 1))
        for t in range(2):

            def sixteen(g, _, t=t):
                r = pl.multiple_of(g * 16, 16)
                d = pl.multiple_of(t * piece + g * 16, 16)

                def store(e, v):
                    nt[pl.ds(d, 16), e * width : (e + 1) * width] = v

                norm_rows(lambda e: xg[e, 2 * n + t, pl.ds(r, 16), :], gb_ref, 1, store, n_ent, width)
                return 0

            lax.fori_loop(0, piece // 16, sixteen, 0)
        part = lax.dot_general(wqb[...], nt[...], (((1,), (1,)), ((), ())), preferred_element_type=F32)
        part = part.astype(BF16)
        for b in range(2 * NY):
            ob[n, b] = part[b * qn : (b + 1) * qn]
        for d in (2, 1, 3, 0):
            for f in range(2):
                result(n, d, f).start()

    def odd(i, lag):
        return lax.div(i - lag, 2)

    local[0].wait()
    start(own(EARLY))
    qs[WD].start()
    start(own(EARLY + 1))
    start([qs[i] for i in (QPA, QMB, QPB, QMA, QD0)])
    for cp in local[1:]:
        cp.wait()
    got([qs[WD]])

    step = min(256, width)

    def tile(i, _):
        @pl.when(i == 3)
        def _():
            got([qs[k] for k in (QPA, QMB, QPB, QMA)])
            start([qs[k] for k in (QPF, QMF, QD1, QD2)])

        @pl.when(i == 5)
        def _():
            got([qs[QPF], qs[QMF]])
            start([qs[QD3A], qs[QD3B]])

        @pl.when(i == 7)
        def _():
            got([qs[k] for k in (QD0, QD1, QD2, QD3A, QD3B)])

        @pl.when((i >= EARLY) & (i < TILES))
        def _():
            got(onward(i))

        @pl.when((i + 1 >= EARLY) & (i + 1 < TILES))
        def _():
            got(own(i + 1))
            start(onward(i + 1))

        @pl.when((i >= 1) & (i + EARLY + 1 < TILES))
        def _():
            start(own(i + EARLY + 1))

        @pl.when(i < TILES)
        def _():
            for h in range(2):
                for col in range(0, width, step):
                    part = jnp.dot(aall[rows(i), :], wdb[h, :, col : col + step], preferred_element_type=F32)
                    for k in range(NY):
                        pbuf[i, h, k, :, col : col + step] = part[k * piece : (k + 1) * piece]
            start(early(i))

        @pl.when((i >= 1) & (i <= TILES))
        def _():
            add_neighbour(i - 1)

        @pl.when((i >= 2) & (i <= TILES + 1))
        def _():
            final(i - 2)

        def extra(k):
            for j in range(TILES):
                if SEND[j] == k:
                    start(next_own(j))
            for n in range(CHUNKS):
                if OUT[n] == k:
                    start(out(n) + [out_own(n)])
            for j in range(TILES):
                if PASS[j] == k:
                    got(next_own(j))
                    start(next_onward(j))
            for n in range(CHUNKS):
                if RELAY[n] == k:
                    got(out_arrived(n))
                    start(relay(n))

        for k in sorted(set(SEND + PASS + OUT + RELAY)):
            pl.when(i == k)(functools.partial(extra, k))

        first, last = 0, 0
        for k in sorted(set(QKV)):
            first = jnp.where(i > k, sum(v <= k for v in QKV), first)
            last = jnp.where(i >= k, sum(v <= k for v in QKV), last)

        def chunk(m, _):
            n = QKV_ORDER[0]
            for k in range(1, CHUNKS):
                n = jnp.where(m == k, QKV_ORDER[k], n)
            qkv(n)
            return 0

        lax.fori_loop(first, last, chunk, 0)
        return 0

    lax.fori_loop(0, STEPS, tile, 0)

    def settle(i, _):
        for cp in early(i) + late(i) + next_own(i) + next_onward(i):
            cp.wait_send()

        @pl.when(i >= EARLY)
        def _():
            for cp in own(i) + onward(i):
                cp.wait_send()

        return 0

    lax.fori_loop(0, TILES, settle, 0)

    def settle_out(n, _):
        for cp in out(n) + list(relay(n)):
            cp.wait_send()
        got([out(n)[-1]] + list(relay(n)))
        out_own(n).wait()
        for d in range(NY):
            for f in range(2):
                result(n, d, f).wait()
        return 0

    lax.fori_loop(0, CHUNKS, settle_out, 0)
    for i in qs:
        qs[i].wait_send()


def solution(mesh):
    assert mesh.shape["row"] == 2 * NX and mesh.shape["col"] == NY
    tok_spec, gain_spec = P("data", "row"), P("row")
    wide_spec, down_spec, qkv_spec = P(None, ("col", "row")), P("col", "row"), P("data", ("col", "row"))

    def params(i):
        return pltpu.CompilerParams(collective_id=i, has_side_effects=True, vmem_limit_bytes=LIMIT)

    def per_device(residual, gain_mlp, gain_attn, w_gate, w_up, w_down, w_qkv):
        tokens, width = residual.shape
        hidden, ff = w_gate.shape
        qn = w_qkv.shape[1]
        half = tokens // 2
        piece = half // PAIRS // 2
        n_ent = 2 * NX
        gains = jnp.concatenate([gain_mlp[None], gain_attn[None], jnp.zeros((6, width), F32)])
        n1 = len(k1_names())
        act, xres, gb, ag = pl.pallas_call(
            k1,
            name="mlp_in",
            out_shape=[
                jax.ShapeDtypeStruct((half, 2 * ff), BF16),
                jax.ShapeDtypeStruct((2, CHUNKS, 2, piece, width), BF16),
                jax.ShapeDtypeStruct((n_ent, 8, width), F32),
                jax.ShapeDtypeStruct((NX, EARLY * NY * piece, 2 * ff), BF16),
            ],
            in_specs=[ANY] * 4,
            out_specs=[VMEM] * 3 + [ANY],
            scratch_shapes=[
                pltpu.VMEM((n_ent, PAIRS, 2, piece, width), BF16),
                pltpu.VMEM((2, hidden, ff), BF16),
                pltpu.VMEM((2, hidden, ff), BF16),
                pltpu.VMEM((2 * piece, hidden), BF16),
                pltpu.VMEM((n_ent, 8, width), F32),
                DMA((n1,)),
                DMA((n1,)),
                DMA((NY + 4,)),
            ],
            compiler_params=params(1),
        )(residual.reshape(2, PAIRS, 2, piece, width), gains, w_gate, w_up)
        resid, qkv_t = pl.pallas_call(
            k2,
            name="mlp_out_qkv",
            out_shape=[
                jax.ShapeDtypeStruct((2, CHUNKS, NY, 2, piece, width), BF16),
                jax.ShapeDtypeStruct((qn, tokens), BF16),
            ],
            in_specs=[ANY, ANY, ANY, VMEM, VMEM, ANY],
            out_specs=[ANY, ANY],
            scratch_shapes=[
                pltpu.VMEM((half, n_ent * ff), BF16),
                pltpu.VMEM((2, n_ent * ff, width), BF16),
                pltpu.VMEM((TILES, 2, NY, piece, width), F32),
                pltpu.VMEM((TILES, 2, piece, width), F32),
                pltpu.VMEM((TILES, 4, piece, width), F32),
                pltpu.VMEM((n_ent, TILES, piece, width), BF16),
                pltpu.VMEM((2 * NY * qn, hidden), BF16),
                pltpu.VMEM((2 * piece, hidden), BF16),
                pltpu.VMEM((CHUNKS, 2 * NY, qn, 2 * piece), BF16),
                DMA((14, TILES)),
                DMA((14, TILES)),
                DMA((12,)),
                DMA((12,)),
                DMA((7, CHUNKS)),
                DMA((7, CHUNKS)),
                DMA((CHUNKS, 2 * NY)),
                DMA((CHUNKS, 2 * NY)),
                DMA((7,)),
                DMA((CHUNKS,)),
                DMA((CHUNKS,)),
            ],
            compiler_params=params(2),
        )(act, ag, w_down, xres, gb, w_qkv.T)
        return resid.reshape(tokens, width), qkv_t.T

    return jax.shard_map(
        per_device,
        mesh=mesh,
        in_specs=(tok_spec, gain_spec, gain_spec, wide_spec, wide_spec, down_spec, wide_spec),
        out_specs=(tok_spec, qkv_spec),
        check_vma=False,
    )
```

time: 794 us -> 278 us (0.35)
  waiting for transfers between devices: 623 us -> 0 us
  Pallas kernels: 0 us -> 270 us
  matrix products: 90.3 us -> 0 us
  blocking collectives: 46.7 us -> 0 us
  other arithmetic: 19.4 us -> 1.37 us
  between operations: 13.8 us -> 0.66 us
    all_gather x3 -> x0, waiting for transfers between devices: 468 us -> none  [the longest x1 158 us: per_device(): normed_full = lax.all_gather(normed, 'row', axis=1, tiled=True)]
    pallas_call x0 -> x2, Pallas kernels: none -> 270 us  [the longest x1 165 us: per_device(): pl.pallas_call(k2, name='mlp_out_qkv', out_shape=[jax.ShapeDtypeStruct((2...]
    psum x1 -> x0, waiting for transfers between devices: 155 us -> none  [per_device(): down_sum = lax.psum(down_part, 'col')]
    dot_general x4 -> x0, matrix products: 90.3 us -> none  [the longest x1 24.9 us: per_device(): down_part = jnp.dot(act_block, w_down, preferred_element_type=jnp.float32)]
    psum x2 -> x0, blocking collectives: 46.7 us -> none  [shard_norm(): sq_total = lax.psum(sq_part, 'row')]
    reduce_sum x2 -> x0, other arithmetic: 11 us -> none  [shard_norm(): sq_part = jnp.sum(shard_f * shard_f, axis=1, keepdims=True)]
    convert_element_type x2 -> x0, other arithmetic: 8.33 us -> none  [shard_norm(): return (shard_f * row_scale * gain).astype(jnp.bfloat16)]
  transfers between devices with their start and end apart: 4 -> 0, of which waited for: 4 -> 0; matrix products, arithmetic and copies ran while one was open for 0% -> 0% of each run, Pallas kernels for 0% -> 0%
where the time goes in v2:
time: 278 us; the launch traced here: 277 us
  Pallas kernels  270 us (97%)
  local copies, waits for them, and re-layouts  5.66 us (2%)
    pallas_call x1, Pallas kernels, per_device(): pl.pallas_call(k2, name='mlp_out_qkv', out_shape=[jax.ShapeDtypeStruct((2...  165 us
    pallas_call x1, Pallas kernels, per_device(): pl.pallas_call(k1, name='mlp_in', out_shape=[jax.ShapeDtypeStruct((half,...  104 us
    unnamed x4, local copies, waits for them, and re-layouts  5.58 us

profile of v2, /device:TPU:97, one launch (start us, length us, event | category | flops | bytes accessed | tf_op | source)
XLA Modules:
  0.0 277.4 jit_solution(13415300596000343377)
XLA Ops:
  0.6 0.1 pad.2.clone
  0.7 1.4 maximum_maximum_fusion.g_ref
  2.1 104.4 %mlp_in.1 = (bf16[2048,1024]{1,0:T(8,128)(2,1)}, bf16[2,4,2,64,512]{4,3,2,1,0:T(8,128)(2,1)}, f32[8,8,512]{2,1,0:T(8,128)}, bf16[4,512,1024]{2,1,0:T(8,128)(2,1)}) custom-call(bf16[2,16,2,64,512]{4,3,2,1,0:T(8,128)(2,1)} %bitcast.6, f32[8,512]{1,0:T(8,128)} %maximum_maximum_fusion.g_ref, bf16[4096,512]{1,0:T(8,128)(2,1)} %wg_ref.1, bf16[4096,512]{1,0:T(8,128)(2,1)} %wu_ref.1), custom_call_target="tpu_custom_call" | custom-call | tf_op jit(solution)/shard_map/mlp_in/pallas_call | solution.py:605
  106.5 165.3 %mlp_out_qkv.1 = (bf16[2,4,4,2,64,512]{5,4,3,2,1,0:T(8,128)(2,1)}, bf16[144,4096]{1,0:T(8,128)(2,1)}) custom-call(bf16[2048,1024]{1,0:T(8,128)(2,1)} %get-tuple-element.8.a_ref, bf16[4,512,1024]{2,1,0:T(8,128)(2,1)} %get-tuple-element.9.ag_ref, bf16[4096,512]{1,0:T(8,128)(2,1)} %wd_ref.1, bf16[2,4,2,64,512]{4,3,2,1,0:T(8,128)(2,1)} %get-tuple-element.10.xres_ref, ...), custom_call_target="tpu_custom_call" | custom-call | tf_op jit(solution)/shard_map/mlp_out_qkv/pallas_call | solution.py:628
  271.8 0.0 copy-start
  271.8 4.6 %copy.11 = bf16[4096,512]{1,0:T(8,128)(2,1)} copy(bf16[4096,512]{1,0:T(8,128)(2,1)} %bitcast.7) | data formatting | bytes 8388608
  276.4 0.0 copy-done
  276.4 1.0 copy.12
  (1 shorter events, 0.0 us)
Async XLA Ops:
  271.8 4.6 %copy-start = (bf16[144,4096]{1,0:T(8,128)(2,1)S(1)}, bf16[144,4096]{1,0:T(8,128)(2,1)}, u32[]{:S(2)}) copy-start(bf16[144,4096]{1,0:T(8,128)(2,1)} %get-tuple-element.13) | copy-start | bytes 3538948

commit v3 on v0

v3 whole, which is shorter than its diff:
```python
import functools

import jax
import jax.numpy as jnp
from jax import lax
from jax.experimental import pallas as pl
from jax.experimental.pallas import tpu as pltpu
from jax.sharding import PartitionSpec as P

NORM_EPS = 1e-6
MESH = pl.DeviceIdType.MESH
BF16 = jnp.bfloat16
F32 = jnp.float32
ANY = pl.BlockSpec(memory_space=pl.ANY)
VMEM = pl.BlockSpec(memory_space=pltpu.VMEM)
DMA = pltpu.SemaphoreType.DMA
LIMIT = 64 * 1024 * 1024 - 128 * 1024

NX, NY = 4, 4
PAIRS = 16
SY = 3
SX = PAIRS - NY * SY
TILES = PAIRS // 2
CHUNKS = TILES // 2
FIRST = NY * SY // 2
SLOTS = 4


def place():
    row, y = lax.axis_index("row"), lax.axis_index("col")
    return lax.div(row, 2), lax.rem(row, 2), row, y


def around(i, n):
    return lax.rem(i + 1, n), lax.rem(i + n - 1, n), lax.rem(i + 2, n)


def greet(peers):
    barrier = pltpu.get_barrier_semaphore()
    for row, y in peers:
        pl.semaphore_signal(barrier, inc=1, device_id={"row": row, "col": y}, device_id_type=MESH)
    pl.semaphore_wait(barrier, len(peers))


def to(src, dst, send, recv, row, y):
    return pltpu.make_async_remote_copy(src, dst, send, recv, device_id={"row": row, "col": y}, device_id_type=MESH)


def start(copies):
    for cp in copies:
        cp.start()


def got(copies):
    for cp in copies:
        cp.wait_recv()


def norm_rows(load, gains, store, n_ent, width):
    acc = None
    for e in range(n_ent):
        v = load(e).astype(F32)
        acc = v * v if acc is None else acc + v * v
    scale = lax.rsqrt(jnp.sum(acc, axis=1, keepdims=True) / (n_ent * width) + NORM_EPS)
    for e in range(n_ent):
        store(e, (load(e).astype(F32) * scale * gains[e]).astype(BF16))


def steps(tokens):
    out, what = [], None
    for token in tokens:
        if token in ("s", "w"):
            what = token
        else:
            out.append((what, token))
    return out


GROUPS = {
    "xp": ("xp", "xm"),
    "xf": ("xpf", "xmf"),
    "ya": ("yp1", "yp2", "ym1", "ym2"),
    "yb": ("yp3", "ym3"),
    "yf": ("ypf1", "ypf3", "ymf2", "ymf3"),
    "s": ("sp", "sm"),
    "sf": ("spf", "smf"),
}
COUNTS = {"xp": SY, "xf": SY, "ya": SY, "yb": SY, "yf": SY, "s": SX, "sf": SX}

IN_TILES = ("x0", "x1", "s0", "p0", "o0", "x2", "x3", "m0", "m1", "s2", "m2", "p1", "p2", "s1", "o1", "o2")
IN_PLAN = (
    ("s", "xp0", "s0", "w", "xp0", "s", "xf0", "w", "s0", "s", "sf0", "s1", "ya0", "xp2", "w", "s1", "s", "sf1", "s2", "xp1", "w", "xf0", "s", "yb0", "w", "xp2", "s", "ya2", "w", "s2", "s", "sf2", "w", "ya0", "yb0", "s", "yf0", "w", "sf0"),
    ("s", "s3", "w", "sf1"),
    (),
    ("w", "xp1", "s", "xf1", "w", "s3", "s", "sf3", "w", "xf1", "s", "yb1", "xf2", "a0", "ya1"),
    ("w", "yf0"),
    ("w", "sf2"),
    ("w", "sf3"),
    ("s", "a1", "w", "xf2", "s", "yb2"),
    ("w", "ya1", "yb1", "s", "yf1", "w", "a0", "s", "af0"),
    (),
    ("w", "ya2", "yb2", "s", "yf2", "q1", "a2"),
    (),
    (),
    (),
    ("w", "a1", "s", "af1", "w", "yf1"),
    ("w", "yf2"),
    ("s", "a3"),
)

ACT = (-1, -1, -1, -1, 1, 2, 3, 4)
SEND = (5, 6, 7, 6, 6, 7, 10, 9)
PASS = (7, 8, 7, 8, 9, 10, 11, 11)
OUT = (2, 4, 4, 5, 7, 8, 8, 9)
RELAY = (2, 4, 5, 5, 10, 11, 11, 11)
QKV = (9, 10, 11, 11)
Q_NEXT, Q_LAST, Q_LOAD = (0, 2, 4)
STEPS = 12
FIRST_S = next(n for n in IN_PLAN[0] if n[0] == "s" and n[1:].isdigit())
QKV_ORDER = tuple(sorted(range(CHUNKS), key=lambda n: (QKV[n], n)))
PASSED = tuple(sum(("s", f"af{i}") in steps(row) for row in IN_PLAN) for i in range(TILES))


def in_names():
    names = []
    for group, parts in GROUPS.items():
        for k in range(COUNTS[group]):
            for part in parts:
                names += [f"{part}{k}a", f"{part}{k}b"] if group == "xp" and k == 0 else [f"{part}{k}"]
    names += [f"d{d}{k}" for d in range(NY) for k in range(SY)] + [f"e{s}" for s in range(2 * SX)]
    names += [f"g{d}{k}" for d in range(1, 2 * NX) for k in range(2)]
    return names + ["wg", "wu", "wd"]


AP, AM, APF, AMF, S1L, S1R, FL, FR, GL, GR, XP, XM, XPF, XMF = range(14)
QPA, QPB, QMB, QMA, QPF, QMF, QD0, QD1, QD2, QD3A, QD3B = range(11)
RP, RM, RPF, RMF, RD = 0, 2, 4, 5, 6


def kernel(
    x_ref, g1_ref, g2_ref, wg_ref, wu_ref, wd_ref, wq_ref, resid_ref, out_ref, wdx_ref, wqa_ref,
    xb, wgb, wub, aall, pbuf, r1, rf, xres, nt, g1b, g2b, ob,
    isend, irecv, send, recv, qsend, qrecv, rsend, rrecv, osend, orecv, loc, rloc, oloc, ready,
):
    x, c, row, y = place()
    xp, xm, x2 = around(x, NX)
    yp, ym, y2 = around(y, NY)
    n_ent = 2 * NX
    width, ff, qn = xb.shape[2], wgb.shape[2], wq_ref.shape[0]
    piece = xb.shape[1] // (2 * PAIRS)
    pair_n, rows_n, ffc = 2 * piece, NY * piece, 2 * ff
    half = PAIRS * pair_n
    row_p, row_m, partner = 2 * xp + c, 2 * xm + c, 2 * x + 1 - c
    ids = {n: i for i, n in enumerate(in_names())}
    copies = {}


    def define(name, src, dst, to_row, to_y):
        i = ids[name]
        copies[name] = to(src, dst, isend.at[i], irecv.at[i], to_row, to_y)

    def circle(name, ents, where, to_row, to_y):
        ref = xb.at[ents, where]
        define(name, ref, ref, to_row, to_y)

    def span(first, n):
        return pl.ds(pl.multiple_of(first * piece, piece), n * piece)

    blk = lambda i: pl.ds(2 * i, 2)
    ent = lambda i: pl.ds(i, 1)
    for k in range(SY):
        where = lambda j: span(2 * (NY * k + j), 2)
        for part, j in (("xp", row_p), ("xm", row_m)):
            if k == 0:
                circle(f"{part}0a", ent(row), where(y), j, y)
                circle(f"{part}0b", ent(partner), where(y), j, y)
            else:
                circle(f"{part}{k}", blk(x), where(y), j, y)
        circle(f"xpf{k}", ent(2 * xm), where(y), row_p, y)
        circle(f"xmf{k}", ent(2 * xp + 1), where(y), row_m, y)
        for tag, j in (("yp", yp), ("ym", ym)):
            for i, b in enumerate((xm, xp, x2)):
                circle(f"{tag}{i + 1}{k}", blk(b), where(y), row, j)
        circle(f"ypf1{k}", blk(xm), where(ym), row, yp)
        circle(f"ypf3{k}", ent(2 * x2), where(ym), row, yp)
        circle(f"ymf2{k}", blk(xp), where(yp), row, ym)
        circle(f"ymf3{k}", ent(2 * x2 + 1), where(yp), row, ym)
    for k in range(SX):
        where = pl.ds((2 * NY * SY + 2 * k) * piece, 2 * piece)
        circle(f"sp{k}", blk(x), where, row_p, y)
        circle(f"sm{k}", blk(x), where, row_m, y)
        circle(f"spf{k}", ent(2 * xm), where, row_p, y)
        circle(f"smf{k}", ent(2 * xp + 1), where, row_m, y)

    local = {}

    def bring(name, i, src_at, dst_at, n):
        there = xb.at[row, span(dst_at, n)]
        mine = pl.ds(pl.multiple_of(c * half + src_at * piece, piece), n * piece)
        theirs = pl.ds(pl.multiple_of((1 - c) * half + src_at * piece, piece), n * piece)
        local[name] = pltpu.make_async_copy(x_ref.at[mine], there, loc.at[i])
        define(name, x_ref.at[theirs], there, partner, y)

    for d in range(NY):
        j = lax.rem(y + d, NY)
        for k in range(SY):
            bring(f"d{d}{k}", d * SY + k, 2 * (NY * k + j), 2 * (NY * k + j), 2)
    for k in range(2 * SX):
        t, p = k // SX, k % SX
        bring(f"e{k}", NY * SY + k, 2 * (NY * SY + p) + t, 2 * NY * SY + k, 1)
    n_loc = NY * SY + 2 * SX
    for d in range(1, n_ent):
        define(f"g{d}0", g1_ref, g1b.at[row], lax.rem(row + d, n_ent), y)
        define(f"g{d}1", g2_ref, g2b.at[row], lax.rem(row + d, n_ent), y)
    define("wg", wg_ref, wgb.at[c], partner, y)
    define("wu", wu_ref, wub.at[c], partner, y)
    define("wd", wd_ref, wdx_ref, partner, y)
    weights = [
        pltpu.make_async_copy(g1_ref, g1b.at[row], loc.at[n_loc]),
        pltpu.make_async_copy(wg_ref, wgb.at[c], loc.at[n_loc + 1]),
        pltpu.make_async_copy(wu_ref, wub.at[c], loc.at[n_loc + 2]),
        pltpu.make_async_copy(g2_ref, g2b.at[row], loc.at[n_loc + 3]),
    ]
    start(local.values())
    start(weights)

    greet(
        [(lax.rem(row + d, n_ent), y) for d in range(1, n_ent)]
        + [(2 * x + h, lax.rem(y + d, NY)) for d in range(1, NY) for h in range(2)]
    )

    copies["d00"].start()
    local["d00"].wait()
    start([copies["xp0a"], copies["xm0a"]])
    own_rows = [f"d0{k}" for k in range(1, SY)]
    round_x = [n for n in local if n[0] == "e"]
    other_rows = [n for n in local if n[0] == "d" and n[1] != "0"]
    start([copies[n] for n in own_rows + round_x])
    start([copies[n] for n in other_rows + [f"g{d}{k}" for d in range(1, n_ent) for k in range(2)] + ["wg", "wu", "wd"]])

    def q(i, ref, to_row, to_y, src=None):
        return to(ref if src is None else src, ref, qsend.at[i], qrecv.at[i], to_row, to_y)

    def wq_at(b, off=0, n=qn):
        return wqa_ref.at[pl.ds(pl.multiple_of(b * qn + off, 16), n)]

    n_a = (qn // 2 + 15) // 16 * 16
    n_b = qn - n_a
    mine, b_m, b_p, b_2 = 2 * y + c, 2 * ym + c, 2 * yp + c, 2 * y2 + c
    src_a, src_b = wq_ref.at[pl.ds(0, n_a)], wq_ref.at[pl.ds(n_a, n_b)]
    qs = {
        QPA: q(QPA, wq_at(mine, 0, n_a), row, yp, src_a),
        QPB: q(QPB, wq_at(mine, n_a, n_b), row, yp, src_b),
        QMB: q(QMB, wq_at(mine, n_a, n_b), row, ym, src_b),
        QMA: q(QMA, wq_at(mine, 0, n_a), row, ym, src_a),
        QPF: q(QPF, wq_at(b_m, 0, n_a), row, yp),
        QMF: q(QMF, wq_at(b_p, n_a, n_b), row, ym),
        QD0: q(QD0, wq_at(mine), partner, y, wq_ref),
        QD1: q(QD1, wq_at(b_m), partner, y),
        QD2: q(QD2, wq_at(b_p), partner, y),
        QD3A: q(QD3A, wq_at(b_2, 0, n_a), partner, y),
        QD3B: q(QD3B, wq_at(b_2, n_a, n_b), partner, y),
    }
    start([qs[QPA], qs[QMB], qs[QD0]])
    got([copies["d00"]])
    start([copies["xp0b"], copies["xm0b"]])
    for n in own_rows:
        local[n].wait()
    got([copies[n] for n in own_rows])
    weights[0].wait()
    for first in range(0, qn, nt.shape[0]):
        n = min(nt.shape[0], qn - first)
        for a, b in ((wq_ref.at[pl.ds(first, n)], nt.at[pl.ds(0, n)]), (nt.at[pl.ds(0, n)], wq_at(mine, first, n))):
            cp = pltpu.make_async_copy(a, b, loc.at[n_loc])
            cp.start()
            cp.wait()

    def cols(i):
        return pl.ds(pl.multiple_of(i * ffc, 128), ffc)

    def at(i):
        return lax.rem(i + FIRST, TILES)

    def chunk_of(n):
        return lax.rem(n + FIRST // 2, CHUNKS)

    def rows(i, off=0, n=rows_n):
        return pl.ds(pl.multiple_of(at(i) * rows_n + off, 16), n)

    def ring(kind, j, src, dst, to_row, to_y):
        return to(src, dst, send.at[kind, j], recv.at[kind, j], to_row, to_y)

    def own(i):
        ref = aall.at[rows(i), cols(x)]
        return ring(AP, i, ref, ref, row_p, y), ring(AM, i, ref, ref, row_m, y)

    def onward(i):
        h = rows_n // 2
        up, down = aall.at[rows(i, 0, h), cols(xm)], aall.at[rows(i, h, h), cols(xp)]
        return ring(APF, i, up, up, row_p, y), ring(AMF, i, down, down, row_m, y)

    def act(tokens):
        for what, token in steps(tokens):
            group, k = token[:-1], int(token[-1])
            if what == "s" and token == FIRST_S:
                for n in round_x:
                    local[n].wait()
                got([copies[n] for n in round_x])
            if group == "q":
                cps = [qs[QPB], qs[QMA]]
            elif group in ("a", "af"):
                cps = own(k) if group == "a" else onward(k)
            else:
                cps = []
                for part in GROUPS[group]:
                    cps += [copies[n] for n in ([f"{part}0a", f"{part}0b"] if token == "xp0" else [f"{part}{k}"])]
            if what == "w":
                got(cps)
            elif token != "xp0":
                start(cps)

    act(IN_PLAN[0])
    for cp in [local[n] for n in other_rows] + weights[1:]:
        cp.wait()
    got([copies[n] for n in other_rows])
    got([copies[n] for n in [f"g{d}{k}" for d in range(1, n_ent) for k in range(2)] + ["wg", "wu"]])

    base = {"s": y, "m": ym, "p": yp, "o": y2}

    def in_tile(s, _):
        for k in range(1, len(IN_TILES)):
            if IN_PLAN[k]:
                pl.when(s == k)(functools.partial(act, IN_PLAN[k]))
        first, p0, p1 = 0, 0, 0
        for k, name in enumerate(IN_TILES):
            i = int(name[1])
            if name[0] == "x":
                where = (2 * NY * SY + 2 * i, 2 * NY * SY + 2 * i, 2 * NY * SY + 2 * i + 1)
            else:
                j = base[name[0]]
                where = (2 * (NY * i + j), 2 * NY * i + j, 2 * NY * i + NY + j)
            first, p0, p1 = (jnp.where(s == k, a, b) for a, b in zip(where, (first, p0, p1)))

        def sixteen(g, _):
            r = pl.multiple_of(first * piece + g * 16, 16)
            d = pl.multiple_of(g * 16, 16)

            def store(e, v):
                nt[pl.ds(d, 16), e * width : (e + 1) * width] = v

            norm_rows(lambda e: xb[e, pl.ds(r, 16), :], g1b, store, n_ent, width)
            return 0

        lax.fori_loop(0, pair_n // 16, sixteen, 0)

        step = min(256, ff)
        for h in range(2):
            for col in range(0, ff, step):
                gate = jnp.dot(nt[...], wgb[h, :, col : col + step], preferred_element_type=F32)
                up = jnp.dot(nt[...], wub[h, :, col : col + step], preferred_element_type=F32)
                act_val = (gate * lax.logistic(gate) * up).astype(BF16)
                there = pl.ds(pl.multiple_of(x * ffc + h * ff + col, 128), step)
                for i, p in enumerate((p0, p1)):
                    aall[pl.ds(pl.multiple_of(p * piece, piece), piece), there] = act_val[i * piece : (i + 1) * piece]
        return 0

    lax.fori_loop(0, len(IN_TILES), in_tile, 0)
    act(IN_PLAN[-1])


    got([copies["wd"]])
    down = [
        pltpu.make_async_copy(wd_ref, wgb.at[c], loc.at[0]),
        pltpu.make_async_copy(wdx_ref, wgb.at[1 - c], loc.at[1]),
    ]
    start(down)
    for j in (row_p, row_m):
        pl.semaphore_signal(ready, inc=1, device_id={"row": j, "col": y}, device_id_type=MESH)
    for i in range(TILES):
        q_at, t = (i + FIRST) % TILES // 2, i % 2
        if q_at * NY < NY * SY:
            first = 2 * (NY * q_at + y) + t
        else:
            first = 2 * NY * SY + t * SX + y
        for h in range(2):
            xres[h, i] = xb[2 * x + h, span(first, 1), :]
    for n in ids:
        copies[n].wait_send()
    for cp in down:
        cp.wait()
    pl.semaphore_wait(ready, 2)


    def early(i):
        slot = lax.rem(i, SLOTS)
        return (
            ring(S1L, i, pbuf.at[slot, 0, y2], r1.at[i, 0], row, yp),
            ring(S1R, i, pbuf.at[slot, 1, y2], r1.at[i, 1], row, ym),
            ring(FR, i, pbuf.at[slot, 1, yp], rf.at[i, 1], row, yp),
            ring(GL, i, pbuf.at[slot, 0, ym], rf.at[i, 2], row, ym),
        )

    def late(i):
        slot = lax.rem(i, SLOTS)
        return (
            ring(FL, i, pbuf.at[slot, 0, yp], rf.at[i, 0], row, yp),
            ring(GR, i, pbuf.at[slot, 1, ym], rf.at[i, 3], row, ym),
        )

    def held(i, e, n=1):
        return wub.at[0, pl.ds(pl.multiple_of((i * n_ent + e) * piece, piece), n * piece)]

    def next_own(i):
        ref = held(i, 2 * x, 2)
        return ring(XP, i, ref, ref, row_p, y), ring(XM, i, ref, ref, row_m, y)

    def next_onward(i):
        up, down = held(i, 2 * xm), held(i, 2 * xp + 1)
        return ring(XPF, i, up, up, row_p, y), ring(XMF, i, down, down, row_m, y)

    def home(i, of_c, of_y):
        return resid_ref.at[of_c, lax.div(at(i), 2), of_y, lax.rem(i, 2)]

    def out(i):
        there = home(i, c, y)
        sends = []
        for h in range(2):
            src = held(i, 2 * x + h)
            sends.append(to(src, there, rsend.at[RP + h, i], rrecv.at[RP + c, i], 2 * x + h, yp))
            sends.append(to(src, there, rsend.at[RM + h, i], rrecv.at[RM + c, i], 2 * x + h, ym))
        sends.append(to(held(i, partner), there, rsend.at[RD, i], rrecv.at[RD, i], partner, y))
        return sends

    def out_own(i):
        return pltpu.make_async_copy(held(i, row), home(i, c, y), rloc.at[i])

    def out_arrived(i):
        return [to(held(i, row), home(i, 0, y), rsend.at[k, i], rrecv.at[k, i], row, yp) for k in range(4)]

    def relay(i):
        up, down = home(i, 0, ym), home(i, 1, yp)
        return (
            to(up, up, rsend.at[RPF, i], rrecv.at[RPF, i], row, yp),
            to(down, down, rsend.at[RMF, i], rrecv.at[RMF, i], row, ym),
        )

    def result(n, d, f):
        h = c if f == 0 else 1 - c
        to_y = lax.rem(y + d, NY)
        src = ob.at[n, 2 * to_y + h]
        first = (c * CHUNKS + chunk_of(n)) * NY + y
        dst = out_ref.at[:, pl.ds(pl.multiple_of(first * pair_n, 128), pair_n)]
        if d == 0 and f == 0:
            return pltpu.make_async_copy(src, dst, oloc.at[n])
        return to(src, dst, osend.at[n, 2 * d + f], orecv.at[n, 2 * d + f], 2 * x + h, to_y)

    def add_neighbour(i):
        got(early(i)[:2])
        slot = lax.rem(i, SLOTS)
        for r in range(0, piece, 16):
            s = pl.ds(r, 16)
            pbuf[slot, 0, yp, s, :] = pbuf[slot, 0, yp, s, :] + r1[i, 0, s, :]
            pbuf[slot, 1, ym, s, :] = pbuf[slot, 1, ym, s, :] + r1[i, 1, s, :]
        start(late(i))

    def final(i):
        got(early(i)[2:] + late(i))
        slot = lax.rem(i, SLOTS)
        for h in range(2):
            ref = held(i, 2 * x + h)
            for r in range(0, piece, 16):
                s = pl.ds(r, 16)
                total = pbuf[slot, h, y, s, :] + rf[i, h, s, :] + rf[i, 2 + h, s, :]
                ref[s, :] = (xres[h, i, s, :].astype(F32) + total).astype(BF16)

    def qkv(n):
        got(next_onward(2 * n) + next_onward(2 * n + 1))
        for t in range(2):

            def sixteen(g, _, t=t):
                r = pl.multiple_of(g * 16, 16)
                d = pl.multiple_of(t * piece + g * 16, 16)

                def store(e, v):
                    nt[pl.ds(d, 16), e * width : (e + 1) * width] = v

                norm_rows(lambda e: held(2 * n + t, e)[pl.ds(r, 16), :], g2b, store, n_ent, width)
                return 0

            lax.fori_loop(0, piece // 16, sixteen, 0)
        for b in range(0, 2 * NY, 2):
            part = None
            for e in range(n_ent):
                lhs, rhs = xb[e, b * qn : (b + 2) * qn, :], nt[:, e * width : (e + 1) * width]
                term = lax.dot_general(lhs, rhs, (((1,), (1,)), ((), ())), preferred_element_type=F32)
                part = term if part is None else part + term
            part = part.astype(BF16)
            for k in range(2):
                ob[n, b + k] = part[k * qn : (k + 1) * qn]
        for d in (2, 1, 3, 0):
            for f in range(2):
                result(n, d, f).start()

    def wq_load(e):
        src = wqa_ref.at[:, pl.ds(e * width, width)]
        return pltpu.make_async_copy(src, xb.at[e, pl.ds(0, 2 * NY * qn)], loc.at[e])

    step = min(256, width)

    def tile(i, _):
        @pl.when(i == Q_NEXT)
        def _():
            got([qs[k] for k in (QPA, QMB, QPB, QMA)])
            start([qs[k] for k in (QPF, QMF, QD1, QD2)])

        @pl.when(i == Q_LAST)
        def _():
            got([qs[QPF], qs[QMF]])
            start([qs[QD3A], qs[QD3B]])

        @pl.when(i == Q_LOAD)
        def _():
            got([qs[k] for k in (QD0, QD1, QD2, QD3A, QD3B)])
            start([wq_load(e) for e in range(n_ent)])

        @pl.when(i == Q_LOAD + 1)
        def _():
            for e in range(n_ent):
                wq_load(e).wait()

        @pl.when(i < TILES)
        def _():
            got(onward(i))

        @pl.when((i + 1 >= sum(PASSED)) & (i + 1 < TILES))
        def _():
            got(own(i + 1))
            start(onward(i + 1))

        for k in sorted(set(ACT)):
            if k >= 0:
                pl.when(i == k)(lambda k=k: [start(own(j)) for j in range(TILES) if ACT[j] == k] and None)

        @pl.when((i >= SLOTS) & (i < TILES))
        def _():
            for cp in early(i - SLOTS) + late(i - SLOTS):
                cp.wait_send()

        @pl.when(i < TILES)
        def _():
            slot = lax.rem(i, SLOTS)
            for h in range(2):
                for col in range(0, width, step):
                    part = jnp.dot(aall[rows(i), :], wgb[h, :, col : col + step], preferred_element_type=F32)
                    for k in range(NY):
                        pbuf[slot, h, k, :, col : col + step] = part[k * piece : (k + 1) * piece]
            start(early(i))

        @pl.when((i >= 1) & (i <= TILES))
        def _():
            add_neighbour(i - 1)

        @pl.when((i >= 2) & (i <= TILES + 1))
        def _():
            final(i - 2)

        def extra(k):
            for j in range(TILES):
                if SEND[j] == k:
                    start(next_own(j))
            for j in range(TILES):
                if OUT[j] == k:
                    start(out(j) + [out_own(j)])
            for j in range(TILES):
                if PASS[j] == k:
                    got(next_own(j))
                    start(next_onward(j))
            for j in range(TILES):
                if RELAY[j] == k:
                    got(out_arrived(j))
                    start(relay(j))

        for k in sorted(set(SEND + PASS + OUT + RELAY)):
            pl.when(i == k)(functools.partial(extra, k))

        first, last = 0, 0
        for k in sorted(set(QKV)):
            first = jnp.where(i > k, sum(v <= k for v in QKV), first)
            last = jnp.where(i >= k, sum(v <= k for v in QKV), last)

        def chunk(m, _):
            n = QKV_ORDER[0]
            for k in range(1, CHUNKS):
                n = jnp.where(m == k, QKV_ORDER[k], n)
            qkv(n)
            return 0

        lax.fori_loop(first, last, chunk, 0)
        return 0

    lax.fori_loop(0, STEPS, tile, 0)

    def settle(i, _):
        for cp in own(i) + onward(i) + next_own(i) + next_onward(i):
            cp.wait_send()
        for cp in out(i) + list(relay(i)):
            cp.wait_send()
        got([out(i)[-1]] + list(relay(i)))
        out_own(i).wait()

        @pl.when(i >= TILES - SLOTS)
        def _():
            for cp in early(i) + late(i):
                cp.wait_send()

        return 0

    lax.fori_loop(0, TILES, settle, 0)

    def settle_out(n, _):
        for d in range(NY):
            for f in range(2):
                result(n, d, f).wait()
        return 0

    lax.fori_loop(0, CHUNKS, settle_out, 0)
    for i in qs:
        qs[i].wait_send()


def hand_over(a_ref, b_ref, a_out, b_out, a_buf, b_buf, a_in_sem, a_out_sem, b_sem):
    n = a_in_sem.shape[0]
    rows = a_ref.shape[0] // n
    part = lambda ref, i: ref.at[pl.ds(i * rows, rows)]
    ins = [pltpu.make_async_copy(part(a_ref, i), part(a_buf, i), a_in_sem.at[i]) for i in range(n)]
    outs = [pltpu.make_async_copy(part(a_buf, i), part(a_out, i), a_out_sem.at[i]) for i in range(n)]
    b_in = pltpu.make_async_copy(b_ref, b_buf, b_sem.at[0])
    b_back = pltpu.make_async_copy(b_buf, b_out, b_sem.at[1])
    start(ins + [b_in])
    for i in range(n):
        ins[i].wait()
        outs[i].start()
    b_in.wait()
    b_back.start()
    for cp in outs + [b_back]:
        cp.wait()


def solution(mesh):
    assert mesh.shape["row"] == 2 * NX and mesh.shape["col"] == NY
    tok_spec, gain_spec = P("data", "row"), P("row")
    wide_spec, down_spec, qkv_spec = P(None, ("col", "row")), P("col", "row"), P("data", ("col", "row"))

    def per_device(residual, gain_mlp, gain_attn, w_gate, w_up, w_down, w_qkv):
        tokens, width = residual.shape
        hidden, ff = w_gate.shape
        qn = w_qkv.shape[1]
        half = tokens // 2
        piece = half // PAIRS // 2
        n_ent = 2 * NX
        n_in = len(in_names())
        resid, qkv_t, _, _ = pl.pallas_call(
            kernel,
            name="mlp_qkv",
            out_shape=[
                jax.ShapeDtypeStruct((2, CHUNKS, NY, 2, piece, width), BF16),
                jax.ShapeDtypeStruct((qn, tokens), BF16),
                jax.ShapeDtypeStruct((n_ent * ff, width), BF16),
                jax.ShapeDtypeStruct((2 * NY * qn, hidden), BF16),
            ],
            in_specs=[ANY] * 7,
            out_specs=[ANY] * 4,
            scratch_shapes=[
                pltpu.VMEM((n_ent, half, width), BF16),
                pltpu.VMEM((2, hidden, ff), BF16),
                pltpu.VMEM((2, hidden, ff), BF16),
                pltpu.VMEM((half, n_ent * ff), BF16),
                pltpu.VMEM((SLOTS, 2, NY, piece, width), F32),
                pltpu.VMEM((TILES, 2, piece, width), F32),
                pltpu.VMEM((TILES, 4, piece, width), F32),
                pltpu.VMEM((2, TILES, piece, width), BF16),
                pltpu.VMEM((2 * piece, hidden), BF16),
                pltpu.VMEM((n_ent, 1, width), F32),
                pltpu.VMEM((n_ent, 1, width), F32),
                pltpu.VMEM((CHUNKS, 2 * NY, qn, 2 * piece), BF16),
                DMA((n_in,)),
                DMA((n_in,)),
                DMA((14, TILES)),
                DMA((14, TILES)),
                DMA((11,)),
                DMA((11,)),
                DMA((7, TILES)),
                DMA((7, TILES)),
                DMA((CHUNKS, 2 * NY)),
                DMA((CHUNKS, 2 * NY)),
                DMA((NY * SY + 2 * SX + 4,)),
                DMA((TILES,)),
                DMA((CHUNKS,)),
                pltpu.SemaphoreType.REGULAR,
            ],
            compiler_params=pltpu.CompilerParams(collective_id=1, has_side_effects=True, vmem_limit_bytes=LIMIT),
        )(residual, gain_mlp[None], gain_attn[None], w_gate, w_up, w_down, w_qkv.T)
        parts = 8
        resid, qkv_t = pl.pallas_call(
            hand_over,
            name="hand_over",
            out_shape=[jax.ShapeDtypeStruct((tokens, width), BF16), jax.ShapeDtypeStruct((qn, tokens), BF16)],
            in_specs=[ANY] * 2,
            out_specs=[ANY] * 2,
            scratch_shapes=[
                pltpu.VMEM((tokens, width), BF16),
                pltpu.VMEM((qn, tokens), BF16),
                DMA((parts,)),
                DMA((parts,)),
                DMA((2,)),
            ],
        )(resid.reshape(tokens, width), qkv_t)
        return resid, qkv_t.T

    return jax.shard_map(
        per_device,
        mesh=mesh,
        in_specs=(tok_spec, gain_spec, gain_spec, wide_spec, wide_spec, down_spec, wide_spec),
        out_specs=(tok_spec, qkv_spec),
        check_vma=False,
    )
```

time: 794 us -> 266 us (0.34)
  waiting for transfers between devices: 623 us -> 0 us
  Pallas kernels: 0 us -> 265 us
  matrix products: 90.3 us -> 0 us
  blocking collectives: 46.7 us -> 0 us
  other arithmetic: 19.4 us -> 0 us
  between operations: 13.8 us -> 0.64 us
    all_gather x3 -> x0, waiting for transfers between devices: 468 us -> none  [the longest x1 158 us: per_device(): normed_full = lax.all_gather(normed, 'row', axis=1, tiled=True)]
    pallas_call x0 -> x2, Pallas kernels: none -> 265 us  [the longest x1 260 us: per_device(): pl.pallas_call(kernel, name='mlp_qkv', out_shape=[jax.ShapeDtypeStruct((2...]
    psum x1 -> x0, waiting for transfers between devices: 155 us -> none  [per_device(): down_sum = lax.psum(down_part, 'col')]
    dot_general x4 -> x0, matrix products: 90.3 us -> none  [the longest x1 24.9 us: per_device(): down_part = jnp.dot(act_block, w_down, preferred_element_type=jnp.float32)]
    psum x2 -> x0, blocking collectives: 46.7 us -> none  [shard_norm(): sq_total = lax.psum(sq_part, 'row')]
    reduce_sum x2 -> x0, other arithmetic: 11 us -> none  [shard_norm(): sq_part = jnp.sum(shard_f * shard_f, axis=1, keepdims=True)]
    convert_element_type x2 -> x0, other arithmetic: 8.33 us -> none  [shard_norm(): return (shard_f * row_scale * gain).astype(jnp.bfloat16)]
  transfers between devices with their start and end apart: 4 -> 0, of which waited for: 4 -> 0; matrix products, arithmetic and copies ran while one was open for 0% -> 0% of each run, Pallas kernels for 0% -> 0%
where the time goes in v3:
time: 266 us
  Pallas kernels  265 us (100%)
    pallas_call x1, Pallas kernels, per_device(): pl.pallas_call(kernel, name='mlp_qkv', out_shape=[jax.ShapeDtypeStruct((2...  260 us

profile of v3, /device:TPU:97, one launch (start us, length us, event | category | flops | bytes accessed | tf_op | source)
XLA Modules:
  0.0 266.0 jit_solution(848809067371635523)
XLA Ops:
  0.6 260.3 %mlp_qkv.1 = (bf16[2,4,4,2,64,512]{5,4,3,2,1,0:T(8,128)(2,1)}, bf16[144,4096]{1,0:T(8,128)(2,1)}, bf16[4096,512]{1,0:T(8,128)(2,1)}, bf16[1152,4096]{1,0:T(8,128)(2,1)}) custom-call(bf16[4096,512]{1,0:T(8,128)(2,1)} %x_ref.1, f32[1,512]{1,0:T(1,128)} %bitcast.7, f32[1,512]{1,0:T(1,128)} %bitcast.8, bf16[4096,512]{1,0:T(8,128)(2,1)} %wg_ref.1, ...), custom_call_target="tpu_custom_call" | custom-call | tf_op jit(solution)/shard_map/mlp_qkv/pallas_call | solution.py:662
  260.9 5.1 %hand_over.1 = (bf16[4096,512]{1,0:T(8,128)(2,1)}, bf16[144,4096]{1,0:T(8,128)(2,1)}) custom-call(bf16[4096,512]{1,0:T(8,128)(2,1)} %bitcast.5, bf16[144,4096]{1,0:T(8,128)(2,1)} %get-tuple-element.7.b_ref), custom_call_target="tpu_custom_call" | custom-call | tf_op jit(solution)/shard_map/hand_over/pallas_call | solution.py:704

commit v4 on v3

--- a/solution.py
+++ b/solution.py
@@ -87,38 +87,89 @@
 }
 COUNTS = {"xp": SY, "xf": SY, "ya": SY, "yb": SY, "yf": SY, "s": SX, "sf": SX}
 
-IN_TILES = ("x0", "x1", "s0", "p0", "o0", "x2", "x3", "m0", "m1", "s2", "m2", "p1", "p2", "s1", "o1", "o2")
+IN_TILES = ("p0", "m0", "s0", "o0", "s1", "x1", "x0", "x2", "x3", "s2", "m1", "o1", "m2", "p1", "p2", "o2")
 IN_PLAN = (
-    ("s", "xp0", "s0", "w", "xp0", "s", "xf0", "w", "s0", "s", "sf0", "s1", "ya0", "xp2", "w", "s1", "s", "sf1", "s2", "xp1", "w", "xf0", "s", "yb0", "w", "xp2", "s", "ya2", "w", "s2", "s", "sf2", "w", "ya0", "yb0", "s", "yf0", "w", "sf0"),
-    ("s", "s3", "w", "sf1"),
-    (),
-    ("w", "xp1", "s", "xf1", "w", "s3", "s", "sf3", "w", "xf1", "s", "yb1", "xf2", "a0", "ya1"),
+    ("s", "xp0", "s2", "xp1", "w", "xp0", "s", "xf0", "s1", "ya0", "w", "xp1", "s", "xf1", "w", "xf0", "s", "yb0", "s3", "w", "ya0", "yb0", "s", "yf0", "w", "s1", "s", "sf1", "xp2"),
+    (),
+    ("s", "ya1", "w", "s2", "s", "sf2", "s0", "w", "xp2", "s", "xf2", "w", "s3", "s", "sf3"),
     ("w", "yf0"),
-    ("w", "sf2"),
+    ("s", "ya2", "w", "xf1"),
+    ("s", "a3", "w", "sf1"),
+    ("w", "s0", "s", "sf0", "w", "xf2", "s", "yb2", "yb1", "a2", "w", "sf0"),
+    ("w", "ya1", "yb1", "s", "yf1", "w", "a3", "s", "af3", "w", "sf2"),
     ("w", "sf3"),
-    ("s", "a1", "w", "xf2", "s", "yb2"),
-    ("w", "ya1", "yb1", "s", "yf1", "w", "a0", "s", "af0"),
-    (),
-    ("w", "ya2", "yb2", "s", "yf2", "q1", "a2"),
-    (),
-    (),
-    (),
-    ("w", "a1", "s", "af1", "w", "yf1"),
-    ("w", "yf2"),
-    ("s", "a3"),
+    ("s", "a1", "q1", "a0"),
+    ("w", "ya2", "yb2", "s", "yf2"),
+    ("w", "yf1"),
+    (),
+    (),
+    (),
+    ("w", "a1", "s", "af1", "w", "a2", "s", "af2", "q2", "w", "a0", "s", "af0", "w", "yf2"),
+    (),
 )
 
-ACT = (-1, -1, -1, -1, 1, 2, 3, 4)
-SEND = (5, 6, 7, 6, 6, 7, 10, 9)
-PASS = (7, 8, 7, 8, 9, 10, 11, 11)
-OUT = (2, 4, 4, 5, 7, 8, 8, 9)
-RELAY = (2, 4, 5, 5, 10, 11, 11, 11)
-QKV = (9, 10, 11, 11)
-Q_NEXT, Q_LAST, Q_LOAD = (0, 2, 4)
-STEPS = 12
+HEAVY = (
+    ("mm", 1),
+    ("mm", 3),
+    ("add", 3),
+    ("add", 1),
+    ("mm", 0),
+    ("mm", 2),
+    ("fin", 1),
+    ("fin", 3),
+    ("add", 0),
+    ("add", 2),
+    ("fin", 0),
+    ("mm", 5),
+    ("fin", 2),
+    ("add", 5),
+    ("fin", 5),
+    ("mm", 4),
+    ("add", 4),
+    ("mm", 6),
+    ("fin", 4),
+    ("add", 6),
+    ("mm", 7),
+    ("fin", 6),
+    ("add", 7),
+    ("fin", 7),
+    ("qkv", 2),
+    ("qkv", 1),
+    ("qkv", 0),
+    ("qkv", 3),
+)
+LIGHT = (
+    ("a5",),
+    ("a4",),
+    (),
+    (),
+    (),
+    (),
+    ("q3", "af5"),
+    ("a6",),
+    (),
+    (),
+    ("out1",),
+    ("out0",),
+    ("relay1", "af4"),
+    (),
+    ("out3", "af6"),
+    ("out5", "a7", "relay0"),
+    ("send5",),
+    (),
+    (),
+    ("out2", "af7", "send4", "send2", "out4", "relay2"),
+    ("q4", "send3"),
+    ("pass4", "pass5", "send1"),
+    ("send0", "out6"),
+    ("relay4", "pass2", "relay3", "relay6", "send6"),
+    ("relay5", "pass3", "pass0", "send7", "out7", "pass1", "q5"),
+    (),
+    ("relay7", "pass7", "pass6"),
+    (),
+)
+KINDS = ("mm", "add", "fin", "qkv")
 FIRST_S = next(n for n in IN_PLAN[0] if n[0] == "s" and n[1:].isdigit())
-QKV_ORDER = tuple(sorted(range(CHUNKS), key=lambda n: (QKV[n], n)))
-PASSED = tuple(sum(("s", f"af{i}") in steps(row) for row in IN_PLAN) for i in range(TILES))
 
 
 def in_names():
@@ -306,8 +357,11 @@
                 for n in round_x:
                     local[n].wait()
                 got([copies[n] for n in round_x])
-            if group == "q":
+            if token == "q1":
                 cps = [qs[QPB], qs[QMA]]
+            elif token == "q2":
+                got([qs[i] for i in (QPA, QMB, QPB, QMA)])
+                cps = [qs[i] for i in (QPF, QMF, QD1, QD2)]
             elif group in ("a", "af"):
                 cps = own(k) if group == "a" else onward(k)
             else:
@@ -507,98 +561,65 @@
 
     step = min(256, width)
 
-    def tile(i, _):
-        @pl.when(i == Q_NEXT)
-        def _():
-            got([qs[k] for k in (QPA, QMB, QPB, QMA)])
-            start([qs[k] for k in (QPF, QMF, QD1, QD2)])
-
-        @pl.when(i == Q_LAST)
-        def _():
-            got([qs[QPF], qs[QMF]])
-            start([qs[QD3A], qs[QD3B]])
-
-        @pl.when(i == Q_LOAD)
-        def _():
-            got([qs[k] for k in (QD0, QD1, QD2, QD3A, QD3B)])
-            start([wq_load(e) for e in range(n_ent)])
-
-        @pl.when(i == Q_LOAD + 1)
-        def _():
-            for e in range(n_ent):
-                wq_load(e).wait()
-
-        @pl.when(i < TILES)
-        def _():
-            got(onward(i))
-
-        @pl.when((i + 1 >= sum(PASSED)) & (i + 1 < TILES))
-        def _():
-            got(own(i + 1))
-            start(onward(i + 1))
-
-        for k in sorted(set(ACT)):
-            if k >= 0:
-                pl.when(i == k)(lambda k=k: [start(own(j)) for j in range(TILES) if ACT[j] == k] and None)
-
-        @pl.when((i >= SLOTS) & (i < TILES))
+    def multiply(i):
+        got(onward(i))
+
+        @pl.when(i >= SLOTS)
         def _():
             for cp in early(i - SLOTS) + late(i - SLOTS):
                 cp.wait_send()
 
-        @pl.when(i < TILES)
-        def _():
-            slot = lax.rem(i, SLOTS)
-            for h in range(2):
-                for col in range(0, width, step):
-                    part = jnp.dot(aall[rows(i), :], wgb[h, :, col : col + step], preferred_element_type=F32)
-                    for k in range(NY):
-                        pbuf[slot, h, k, :, col : col + step] = part[k * piece : (k + 1) * piece]
-            start(early(i))
-
-        @pl.when((i >= 1) & (i <= TILES))
-        def _():
-            add_neighbour(i - 1)
-
-        @pl.when((i >= 2) & (i <= TILES + 1))
-        def _():
-            final(i - 2)
-
-        def extra(k):
-            for j in range(TILES):
-                if SEND[j] == k:
-                    start(next_own(j))
-            for j in range(TILES):
-                if OUT[j] == k:
-                    start(out(j) + [out_own(j)])
-            for j in range(TILES):
-                if PASS[j] == k:
-                    got(next_own(j))
-                    start(next_onward(j))
-            for j in range(TILES):
-                if RELAY[j] == k:
-                    got(out_arrived(j))
-                    start(relay(j))
-
-        for k in sorted(set(SEND + PASS + OUT + RELAY)):
-            pl.when(i == k)(functools.partial(extra, k))
-
-        first, last = 0, 0
-        for k in sorted(set(QKV)):
-            first = jnp.where(i > k, sum(v <= k for v in QKV), first)
-            last = jnp.where(i >= k, sum(v <= k for v in QKV), last)
-
-        def chunk(m, _):
-            n = QKV_ORDER[0]
-            for k in range(1, CHUNKS):
-                n = jnp.where(m == k, QKV_ORDER[k], n)
-            qkv(n)
-            return 0
-
-        lax.fori_loop(first, last, chunk, 0)
+        slot = lax.rem(i, SLOTS)
+        for h in range(2):
+            for col in range(0, width, step):
+                part = jnp.dot(aall[rows(i), :], wgb[h, :, col : col + step], preferred_element_type=F32)
+                for k in range(NY):
+                    pbuf[slot, h, k, :, col : col + step] = part[k * piece : (k + 1) * piece]
+        start(early(i))
+
+    def light(tokens):
+        for token in tokens:
+            name, j = token[:-1], int(token[-1])
+            if name == "a":
+                start(own(j))
+            elif name == "af":
+                got(own(j))
+                start(onward(j))
+            elif name == "send":
+                start(next_own(j))
+            elif name == "pass":
+                got(next_own(j))
+                start(next_onward(j))
+            elif name == "out":
+                start(out(j) + [out_own(j)])
+            elif name == "relay":
+                got(out_arrived(j))
+                start(relay(j))
+            elif token == "q3":
+                got([qs[QPF], qs[QMF]])
+                start([qs[QD3A], qs[QD3B]])
+            elif token == "q4":
+                got([qs[k] for k in (QD0, QD1, QD2, QD3A, QD3B)])
+                start([wq_load(e) for e in range(n_ent)])
+            elif token == "q5":
+                for e in range(n_ent):
+                    wq_load(e).wait()
+
+    bodies = {"mm": multiply, "add": add_neighbour, "fin": final, "qkv": qkv}
+
+    def out_step(s, _):
+        for k, tokens in enumerate(LIGHT):
+            if tokens:
+                pl.when(s == k)(functools.partial(light, tokens))
+        kind, j = KINDS.index(HEAVY[0][0]), HEAVY[0][1]
+        for k, (name, i) in enumerate(HEAVY[1:]):
+            kind = jnp.where(s == k + 1, KINDS.index(name), kind)
+            j = jnp.where(s == k + 1, i, j)
+        for k, name in enumerate(KINDS):
+            pl.when(kind == k)(functools.partial(bodies[name], j))
         return 0
 
-    lax.fori_loop(0, STEPS, tile, 0)
+    lax.fori_loop(0, len(HEAVY), out_step, 0)
 
     def settle(i, _):
         for cp in own(i) + onward(i) + next_own(i) + next_onward(i):
@@ -700,7 +721,7 @@
             ],
             compiler_params=pltpu.CompilerParams(collective_id=1, has_side_effects=True, vmem_limit_bytes=LIMIT),
         )(residual, gain_mlp[None], gain_attn[None], w_gate, w_up, w_down, w_qkv.T)
-        parts = 8
+        parts = 2
         resid, qkv_t = pl.pallas_call(
             hand_over,
             name="hand_over",

time: 266 us -> 258 us (0.970)
  Pallas kernels: 265 us -> 257 us
    pallas_call x1, Pallas kernels: 260 us -> 253 us  [per_device(): pl.pallas_call(kernel, name='mlp_qkv', out_shape=[jax.ShapeDtypeStruct((2...]
where the time goes in v4:
time: 258 us
  Pallas kernels  257 us (100%)
    pallas_call x1, Pallas kernels, per_device(): pl.pallas_call(kernel, name='mlp_qkv', out_shape=[jax.ShapeDtypeStruct((2...  253 us

profile of v4, /device:TPU:97, one launch (start us, length us, event | category | flops | bytes accessed | tf_op | source)
XLA Modules:
  0.0 258.0 jit_solution(17353662966159985381)
XLA Ops:
  0.6 253.4 %mlp_qkv.1 = (bf16[2,4,4,2,64,512]{5,4,3,2,1,0:T(8,128)(2,1)}, bf16[144,4096]{1,0:T(8,128)(2,1)}, bf16[4096,512]{1,0:T(8,128)(2,1)}, bf16[1152,4096]{1,0:T(8,128)(2,1)}) custom-call(bf16[4096,512]{1,0:T(8,128)(2,1)} %x_ref.1, f32[1,512]{1,0:T(1,128)} %bitcast.7, f32[1,512]{1,0:T(1,128)} %bitcast.8, bf16[4096,512]{1,0:T(8,128)(2,1)} %wg_ref.1, ...), custom_call_target="tpu_custom_call" | custom-call | tf_op jit(solution)/shard_map/mlp_qkv/pallas_call | solution.py:683
  254.0 4.0 %hand_over.1 = (bf16[4096,512]{1,0:T(8,128)(2,1)}, bf16[144,4096]{1,0:T(8,128)(2,1)}) custom-call(bf16[4096,512]{1,0:T(8,128)(2,1)} %bitcast.5, bf16[144,4096]{1,0:T(8,128)(2,1)} %get-tuple-element.7.b_ref), custom_call_target="tpu_custom_call" | custom-call | tf_op jit(solution)/shard_map/hand_over/pallas_call | solution.py:725

commit v5 on v4

--- a/solution.py
+++ b/solution.py
@@ -87,42 +87,42 @@
 }
 COUNTS = {"xp": SY, "xf": SY, "ya": SY, "yb": SY, "yf": SY, "s": SX, "sf": SX}
 
-IN_TILES = ("p0", "m0", "s0", "o0", "s1", "x1", "x0", "x2", "x3", "s2", "m1", "o1", "m2", "p1", "p2", "o2")
+IN_TILES = ("p0", "m0", "s1", "s0", "o0", "x1", "s2", "x2", "x0", "x3", "o1", "p2", "m1", "p1", "m2", "o2")
 IN_PLAN = (
-    ("s", "xp0", "s2", "xp1", "w", "xp0", "s", "xf0", "s1", "ya0", "w", "xp1", "s", "xf1", "w", "xf0", "s", "yb0", "s3", "w", "ya0", "yb0", "s", "yf0", "w", "s1", "s", "sf1", "xp2"),
-    (),
-    ("s", "ya1", "w", "s2", "s", "sf2", "s0", "w", "xp2", "s", "xf2", "w", "s3", "s", "sf3"),
+    ("s", "xp0", "s1", "s2", "w", "xp0", "s", "xf0", "xp1", "ya0", "s3", "w", "xf0", "s", "yb0", "w", "xp1", "s", "xf1", "w", "s1", "s", "sf1", "xp2", "w", "ya0", "yb0", "s", "yf0", "w", "s3", "s", "sf3"),
+    ("s", "ya1"),
+    ("s", "s0", "w", "s2", "s", "sf2", "w", "xf1"),
+    (),
     ("w", "yf0"),
-    ("s", "ya2", "w", "xf1"),
-    ("s", "a3", "w", "sf1"),
-    ("w", "s0", "s", "sf0", "w", "xf2", "s", "yb2", "yb1", "a2", "w", "sf0"),
-    ("w", "ya1", "yb1", "s", "yf1", "w", "a3", "s", "af3", "w", "sf2"),
-    ("w", "sf3"),
-    ("s", "a1", "q1", "a0"),
-    ("w", "ya2", "yb2", "s", "yf2"),
-    ("w", "yf1"),
-    (),
-    (),
-    (),
-    ("w", "a1", "s", "af1", "w", "a2", "s", "af2", "q2", "w", "a0", "s", "af0", "w", "yf2"),
-    (),
+    ("w", "xp2", "s", "xf2", "a3", "ya2", "w", "sf1"),
+    ("w", "xf2"),
+    ("w", "s0", "s", "sf0", "yb1", "a2", "yb2", "w", "ya1", "yb1", "s", "yf1", "w", "sf2"),
+    ("w", "sf0"),
+    ("w", "a3", "s", "af3", "w", "sf3"),
+    ("s", "a1", "q1", "a0", "w", "ya2", "yb2", "s", "yf2", "w", "yf1"),
+    (),
+    (),
+    ("w", "a1", "s", "af1", "w", "a2", "s", "af2"),
+    ("s", "q2"),
+    ("w", "yf2"),
+    ("w", "a0", "s", "af0"),
 )
 
 HEAVY = (
     ("mm", 1),
     ("mm", 3),
-    ("add", 3),
     ("add", 1),
     ("mm", 0),
+    ("add", 3),
     ("mm", 2),
     ("fin", 1),
-    ("fin", 3),
     ("add", 0),
     ("add", 2),
+    ("fin", 3),
     ("fin", 0),
     ("mm", 5),
+    ("add", 5),
     ("fin", 2),
-    ("add", 5),
     ("fin", 5),
     ("mm", 4),
     ("add", 4),
@@ -140,32 +140,32 @@
 )
 LIGHT = (
     ("a5",),
+    (),
+    (),
     ("a4",),
-    (),
-    (),
     (),
     (),
     ("q3", "af5"),
     ("a6",),
     (),
-    (),
     ("out1",),
-    ("out0",),
-    ("relay1", "af4"),
+    (),
+    ("af4", "out0"),
     (),
     ("out3", "af6"),
-    ("out5", "a7", "relay0"),
+    (),
+    ("a7", "out5", "relay0"),
+    ("relay1",),
     ("send5",),
     (),
-    (),
-    ("out2", "af7", "send4", "send2", "out4", "relay2"),
-    ("q4", "send3"),
-    ("pass4", "pass5", "send1"),
-    ("send0", "out6"),
-    ("relay4", "pass2", "relay3", "relay6", "send6"),
-    ("relay5", "pass3", "pass0", "send7", "out7", "pass1", "q5"),
-    (),
-    ("relay7", "pass7", "pass6"),
+    ("af7", "send4", "out2", "send2", "out4", "send3"),
+    ("q4", "relay2", "send1"),
+    ("pass5", "pass4"),
+    ("send0", "out6", "pass2"),
+    ("send6", "pass3", "relay3", "relay4", "relay6"),
+    ("relay5", "send7", "pass0", "out7", "pass1", "q5"),
+    ("pass6",),
+    ("relay7", "pass7"),
     (),
 )
 KINDS = ("mm", "add", "fin", "qkv")

time: 258 us -> 258 us (level)
  no operation moved by 1% of the time
where the time goes in v5:
time: 258 us
  Pallas kernels  257 us (100%)
    pallas_call x1, Pallas kernels, per_device(): pl.pallas_call(kernel, name='mlp_qkv', out_shape=[jax.ShapeDtypeStruct((2...  253 us

profile of v5, /device:TPU:97, one launch (start us, length us, event | category | flops | bytes accessed | tf_op | source)
XLA Modules:
  0.0 258.0 jit_solution(4154172794028555659)
XLA Ops:
  0.6 253.3 %mlp_qkv.1 = (bf16[2,4,4,2,64,512]{5,4,3,2,1,0:T(8,128)(2,1)}, bf16[144,4096]{1,0:T(8,128)(2,1)}, bf16[4096,512]{1,0:T(8,128)(2,1)}, bf16[1152,4096]{1,0:T(8,128)(2,1)}) custom-call(bf16[4096,512]{1,0:T(8,128)(2,1)} %x_ref.1, f32[1,512]{1,0:T(1,128)} %bitcast.7, f32[1,512]{1,0:T(1,128)} %bitcast.8, bf16[4096,512]{1,0:T(8,128)(2,1)} %wg_ref.1, ...), custom_call_target="tpu_custom_call" | custom-call | tf_op jit(solution)/shard_map/mlp_qkv/pallas_call | solution.py:683
  253.9 4.0 %hand_over.1 = (bf16[4096,512]{1,0:T(8,128)(2,1)}, bf16[144,4096]{1,0:T(8,128)(2,1)}) custom-call(bf16[4096,512]{1,0:T(8,128)(2,1)} %bitcast.5, bf16[144,4096]{1,0:T(8,128)(2,1)} %get-tuple-element.7.b_ref), custom_call_target="tpu_custom_call" | custom-call | tf_op jit(solution)/shard_map/hand_over/pallas_call | solution.py:725
